TPU v7x, 32 devices: a whole 2x2x4 slice. The times are simulated.
32 devices in a mesh: wall: 8 (over y, x, core), span: 4 (over z).
Axes of the slice: x: 2, y: 2, z: 4, core: 2. Of those that a mesh axis runs over, the one named last changes fastest.
Arguments:
- velocity_old: float32 [3, 128, 64, 128], P(None, 'wall', 'span'), may hold values from -12 to 12, as said below
- heights: float32 [16], replicated, may hold values from 0.04 to 0.25
- owner_device: int32 [16384, 1], P(('wall', 'span')), may hold values from 0 to 7, as said below
- owner_element: int32 [16384, 1], P(('wall', 'span')), may hold values from 0 to 63, as said below
- ref_coords: float32 [3, 16384], P(None, ('wall', 'span')), may hold values from -1 to 1
- roughness: float32 [16384], P(('wall', 'span')), may hold values from 0.0001 to 0.01
Outputs:
- velocity_new: float32 [3, 128, 64, 128], P(None, 'wall', 'span')
- neumann: float32 [2, 16384], P(None, ('wall', 'span'))
Inputs may be any that keep to these rules, and one draw needn't show every extreme that they name: `velocity_old`: values at coinciding nodes of neighbouring elements are equal. `owner_device`: the owner is the streamwise index w of the point's own device, or w + 1 or w - 1 modulo 8. Among the rows of one device at most 128 name w + 1 and at most 128 name w - 1; some device has exactly 128 for w + 1 and some device exactly 128 for w - 1. `owner_element`: the element index is (ex * 2 + ez) * 16 + ey with ex = i // 8 and ez = j // 8 of the wall point; ey < 2 for points of the first wall, ey >= 14 for the second.
All inputs are finite; a program needn't handle non-finite values.
Results may differ from a plain program's by a relative error of at most 0.0003.
Values sent between devices are 32-bit elements; how exact they have to be, the bound alone decides.
A program may use at most 128 MiB of HBM per device.

v0:
```python
import math

import jax
import jax.numpy as jnp
import numpy as np
from jax import lax
from jax.sharding import PartitionSpec as P

ITERS = 3


GLL_NODES = (
    -1.0,
    -0.8717401485096066,
    -0.5917001814331423,
    -0.2092992179024789,
    0.2092992179024789,
    0.5917001814331423,
    0.8717401485096066,
    1.0,
)
GLL_WEIGHTS = (
    0.03571428571428571,
    0.2107042271435061,
    0.3411226924835044,
    0.4124587946587038,
    0.4124587946587038,
    0.3411226924835044,
    0.2107042271435061,
    0.03571428571428571,
)
viscosity = 0.02
inverse_step = 20.0
karman = 0.41
sample_height = 0.1
speed_floor = 0.01
element_dx = 0.05
element_dz = 0.13
precise = lax.Precision.HIGHEST


def with_halo(cells, sides, width):
    for axis, dim in sides:
        count = lax.axis_size(axis)
        head = lax.slice_in_dim(cells, 0, width, axis=dim)
        tail = lax.slice_in_dim(cells, cells.shape[dim] - width, cells.shape[dim], axis=dim)
        cells = jnp.concatenate(
            [
                lax.ppermute(tail, axis, [(i, (i + 1) % count) for i in range(count)]),
                cells,
                lax.ppermute(head, axis, [((i + 1) % count, i) for i in range(count)]),
            ],
            axis=dim,
        )
    return cells


def shifted(value, axis, steps):
    count = lax.axis_size(axis)
    pairs = [(source, (source + steps) % count) for source in range(count)]
    return lax.ppermute(value, axis, pairs)


def stiffness_table():
    points = np.array(GLL_NODES)
    weights = np.array(GLL_WEIGHTS)
    previous = np.ones(8)
    current = points.copy()
    for degree in range(1, 7):
        previous, current = (
            current,
            ((2 * degree + 1) * points * current - degree * previous) / (degree + 1),
        )
    derivative = np.zeros((8, 8))
    for target in range(8):
        for source in range(8):
            if target != source:
                derivative[target, source] = (
                    current[target] / current[source] / (points[target] - points[source])
                )
    derivative[0, 0] = -14.0
    derivative[7, 7] = 14.0
    return derivative.T @ (weights[:, None] * derivative)


def lagrange(coord):
    points = np.array(GLL_NODES)
    gaps_table = points[:, None] - points[None, :] + np.eye(8)
    scale_row = jnp.asarray(1.0 / np.prod(gaps_table, axis=1), jnp.float32)
    gaps = coord[:, None] - jnp.asarray(points, jnp.float32)[None, :]
    filled = jnp.where(jnp.asarray(np.eye(8) > 0.5)[None], jnp.float32(1.0), gaps[:, None, :])
    return jnp.prod(filled, axis=2) * scale_row[None, :]


def face_weights(length, open_ends):
    values = np.ones(length)
    position = np.arange(length) % 8
    values[(position == 0) | (position == 7)] = 0.5
    if open_ends:
        values[0] = 1.0
        values[-1] = 1.0
    return values


def join_faces(core, before, after, axis):
    count = core.shape[axis] // 8
    blocks = core.reshape(core.shape[:axis] + (count, 8) + core.shape[axis + 1 :])
    first = lax.slice_in_dim(blocks, 0, 1, axis=axis + 1)
    last = lax.slice_in_dim(blocks, 7, 8, axis=axis + 1)
    before_b = jnp.expand_dims(before, axis + 1)
    after_b = jnp.expand_dims(after, axis + 1)
    prev_last = jnp.concatenate([before_b, lax.slice_in_dim(last, 0, count - 1, axis=axis)], axis)
    next_first = jnp.concatenate([lax.slice_in_dim(first, 1, count, axis=axis), after_b], axis)
    middle = lax.slice_in_dim(blocks, 1, 7, axis=axis + 1)
    joined = jnp.concatenate([first + prev_last, middle, last + next_first], axis + 1)
    return joined.reshape(core.shape)


def assemble(local):
    padded = with_halo(local, (("wall", 1), ("span", 2)), 1)
    joined_x = join_faces(padded[:, 1:-1], padded[:, :1], padded[:, -1:], 1)
    joined_z = join_faces(joined_x[:, :, 1:-1], joined_x[:, :, :1], joined_x[:, :, -1:], 2)
    border = jnp.zeros(joined_z.shape[:3] + (1,), jnp.float32)
    return join_faces(joined_z, border, border, 3)


def paired_total(first, second):
    return lax.psum((first, second), ("wall", "span"))


def spread(values):
    return values[:, None, None, None]


def slot_numbers(selected, capacity):
    ranking = jnp.cumsum(selected.astype(jnp.int32)) - 1
    return jnp.where(selected, ranking, capacity)


def body(velocity_old, heights, owner_device, owner_element, ref_coords, roughness):
    weights = np.array(GLL_WEIGHTS)
    stiffness = stiffness_table()
    length_x, length_z, length_y = (
        velocity_old.shape[1],
        velocity_old.shape[2],
        velocity_old.shape[3],
    )
    count_x, count_z, count_y = (length_x // 8, length_z // 8, length_y // 8)
    stiff_x = jnp.asarray(np.kron(np.eye(count_x), stiffness * (2.0 / element_dx)), jnp.float32)
    stiff_z = jnp.asarray(np.kron(np.eye(count_z), stiffness * (2.0 / element_dz)), jnp.float32)
    blocks = (2.0 / heights)[:, None, None] * jnp.asarray(stiffness, jnp.float32)[None]
    stiff_y = jnp.einsum("ef,eab->eafb", jnp.eye(count_y, dtype=jnp.float32), blocks).reshape(
        length_y, length_y
    )
    mass_x = jnp.asarray(np.tile(0.5 * element_dx * weights, count_x), jnp.float32)
    mass_z = jnp.asarray(np.tile(0.5 * element_dz * weights, count_z), jnp.float32)
    mass_y = (0.5 * heights[:, None] * jnp.asarray(weights, jnp.float32)[None, :]).reshape(length_y)
    mass_xb = mass_x[None, :, None, None]
    mass_zb = mass_z[None, None, :, None]
    mass_yb = mass_y[None, None, None, :]
    mass_all = mass_xb * mass_zb * mass_yb
    inverse_count = jnp.asarray(
        face_weights(length_x, False)[:, None, None]
        * face_weights(length_z, False)[None, :, None]
        * face_weights(length_y, True)[None, None, :],
        jnp.float32,
    )

    def operate(field):
        along_x = jnp.einsum("ab,cbzy->cazy", stiff_x, field, precision=precise)
        along_z = jnp.einsum("ab,cxby->cxay", stiff_z, field, precision=precise)
        along_y = jnp.einsum("cxzb,ab->cxza", field, stiff_y, precision=precise)
        local = (
            viscosity
            * (
                along_x * mass_zb * mass_yb
                + mass_xb * along_z * mass_yb
                + mass_xb * mass_zb * along_y
            )
            + inverse_step * mass_all * field
        )
        return assemble(local)

    def weighted(first, second):
        return jnp.sum(first * second * inverse_count[None], axis=(1, 2, 3))

    element_rows = (
        velocity_old.reshape(3, count_x, 8, count_z, 8, count_y, 8)
        .transpose(1, 3, 5, 0, 2, 4, 6)
        .reshape(count_x * count_z * count_y, 3 * 512)
    )

    def interpolate(ids_in, coords_in):
        point_total = ids_in.shape[0]
        groups = math.gcd(point_total, 8)
        grouped_ids = ids_in.reshape(groups, point_total // groups)
        grouped_coords = coords_in.T.reshape(groups, point_total // groups, 3)

        def evaluate(pieces):
            row_ids, coords = pieces
            values = element_rows[row_ids].reshape(row_ids.shape[0], 3, 8, 8, 8)
            return jnp.einsum(
                "gcabd,ga,gb,gd->gc",
                values,
                lagrange(coords[:, 0]),
                lagrange(coords[:, 1]),
                lagrange(coords[:, 2]),
                precision=precise,
            )

        result = lax.map(evaluate, (grouped_ids, grouped_coords))
        return result.reshape(point_total, 3).T

    wall_count = lax.axis_size("wall")
    point_count = owner_device.shape[0]
    capacity = point_count // 4
    own_wall = lax.axis_index("wall")
    distance = (owner_device[:, 0] - own_wall + wall_count) % wall_count
    to_next = distance == 1
    to_prev = distance == wall_count - 1
    slot_next = slot_numbers(to_next, capacity)
    slot_prev = slot_numbers(to_prev, capacity)
    packed = jnp.concatenate([owner_element[:, 0].astype(jnp.float32)[None], ref_coords], axis=0)
    empty_buffer = jnp.zeros((4, capacity + 1), jnp.float32)
    send_next = empty_buffer.at[:, slot_next].set(packed)[:, :capacity]
    send_prev = empty_buffer.at[:, slot_prev].set(packed)[:, :capacity]
    got_next = shifted(send_next, "wall", 1)
    got_prev = shifted(send_prev, "wall", -1)
    answer_next = interpolate(got_next[0].astype(jnp.int32), got_next[1:])
    answer_prev = interpolate(got_prev[0].astype(jnp.int32), got_prev[1:])
    back_next = shifted(answer_next, "wall", -1)
    back_prev = shifted(answer_prev, "wall", 1)
    own_values = interpolate(owner_element[:, 0], ref_coords)
    zero_column = jnp.zeros((3, 1), jnp.float32)
    from_next = jnp.concatenate([back_next, zero_column], axis=1)[:, slot_next]
    from_prev = jnp.concatenate([back_prev, zero_column], axis=1)[:, slot_prev]
    velocity_pts = jnp.where(
        to_next[None], from_next, jnp.where(to_prev[None], from_prev, own_values)
    )
    stream = velocity_pts[0]
    spanwise = velocity_pts[2]
    wall_speed = jnp.sqrt(stream * stream + spanwise * spanwise + speed_floor)
    drag_coeff = (karman / jnp.log(sample_height / roughness)) ** 2
    neumann = -(drag_coeff * wall_speed / viscosity)[None, :] * jnp.stack([stream, spanwise])
    traction = (viscosity * neumann).reshape(2, 2, length_x, length_z) * (
        mass_x[:, None] * mass_z[None, :]
    )[None, None]
    zero_plane = jnp.zeros((1, length_x, length_z), jnp.float32)
    bottom = jnp.concatenate([traction[0:1, 0], zero_plane, traction[1:2, 0]], axis=0)
    top_wall = jnp.concatenate([traction[0:1, 1], zero_plane, traction[1:2, 1]], axis=0)
    forcing = inverse_step * mass_all * velocity_old
    forcing = forcing.at[:, :, :, 0].add(bottom).at[:, :, :, -1].add(top_wall)
    right_side = assemble(forcing)
    solution = jnp.zeros_like(right_side)
    residual = right_side
    applied = operate(residual)
    norm_now, product = paired_total(weighted(residual, residual), weighted(residual, applied))
    step_size = norm_now / product
    direction = residual
    along_dir = applied
    for sweep in range(ITERS):
        solution = solution + spread(step_size) * direction
        residual = residual - spread(step_size) * along_dir
        if sweep + 1 < ITERS:
            applied = operate(residual)
            norm_next, product = paired_total(
                weighted(residual, residual), weighted(residual, applied)
            )
            growth = norm_next / norm_now
            step_size = norm_next / (product - growth * norm_next / step_size)
            direction = residual + spread(growth) * direction
            along_dir = applied + spread(growth) * along_dir
            norm_now = norm_next
    return (solution, neumann)


def solution(mesh):
    placed = (
        P(None, "wall", "span", None),
        P(),
        P(("wall", "span"), None),
        P(("wall", "span"), None),
        P(None, ("wall", "span")),
        P(("wall", "span")),
    )
    return jax.shard_map(
        body,
        mesh=mesh,
        in_specs=placed,
        out_specs=(P(None, "wall", "span", None), P(None, ("wall", "span"))),
        check_vma=False,
    )
```

profile of v0, /device:TPU:0, one launch (start us, length us, event | category | flops | bytes accessed | tf_op | source)
XLA Modules:
  0.0 405.2 jit_solution(9068878765870258537)
XLA Ops:
  5.4 1.7 scatter_custom_fusion.1
  7.2 3.4 collective-permute-start.2
  11.2 1.7 scatter_custom_fusion
  15.4 5.9 %reshape.740 = f32[3,2,8,2,8,16,8]{6,5,4,3,2,1,0:T(8,128)} reshape(f32[3,16,16,128]{3,2,1,0:T(8,128)} %param.50) | data formatting | bytes 786432 | tf_op jit(solution)/shard_map/reshape | solution.py:188
  21.6 6.8 %copy.466 = f32[2,2,16,3,8,8,8]{2,1,0,6,5,4,3:T(2,128)} copy(f32[2,2,16,3,8,8,8]{6,2,5,1,4,0,3:T(8,128)} %bitcast.359) | data formatting | bytes 786432 | tf_op jit(solution)/shard_map/transpose | solution.py:189
  28.5 4.0 reshape.741
  32.7 18.7 %while.40 = (s32[]{:T(128)}, f32[8,64,3]{1,0,2:T(8,128)S(1)}, f32[8,64,3]{1,0,2:T(8,128)S(1)}, s32[8,64]{1,0:T(8,128)S(1)}, f32[64,1536]{1,0:T(8,128)S(1)}, /*in...) while((s32[]{:T(128)}, f32[8,64,3]{1,0,2:T(8,128)S(1)}, ...), condition=%wide.region_20.21_spmd.clone.clone, body=%wide.region_16.20_spmd.sunk.clone.clone.sunk | while | flops 229378 | bytes 2121465 | solution.py:211
  52.4 15.5 %while.39 = (s32[]{:T(128)}, f32[8,16,3]{1,2,0:T(4,128)S(1)}, f32[8,16,3]{1,2,0:T(4,128)S(1)}, s32[8,16]{1,0:T(8,128)S(1)}, f32[64,1536]{1,0:T(8,128)S(1)}, /*in...) while((s32[]{:T(128)}, f32[8,16,3]{1,2,0:T(4,128)S(1)}, ...), condition=%wide.region_15.16_spmd.clone.clone, body=%wide.region_11.15_spmd.sunk.clone.clone.sunk | while | flops 58114 | bytes 536561 | solution.py:211
  67.9 15.5 %while.38 = (s32[]{:T(128)}, f32[8,16,3]{1,2,0:T(4,128)S(1)}, f32[8,16,3]{1,2,0:T(4,128)S(1)}, s32[8,16]{1,0:T(8,128)S(1)}, f32[64,1536]{1,0:T(8,128)S(1)}, /*in...) while((s32[]{:T(128)}, f32[8,16,3]{1,2,0:T(4,128)S(1)}, ...), condition=%wide.region_7.8_spmd.clone.clone, body=%wide.region_3.7_spmd.sunk.clone.clone.sunk | while | flops 58114 | bytes 536561 | solution.py:211
  83.7 2.9 collective-permute-start.1
  86.8 1.7 collective-permute-done.1
  93.1 3.1 scatter-add.6
  96.4 6.2 %scatter-add.9 = f32[3,16,16,128]{3,1,2,0:T(8,128)S(1)} dynamic-update-slice(f32[3,16,16,128]{3,1,2,0:T(8,128)S(1)} %scatter-add.6, f32[3,16,16,1]{3,1,2,0:T(8,128)S(1)} %slice_add_fusion.8, s32[]{:T(128)} %constant.175.clone.1, s32[]{:T(128)} %constant.175.clone.1, s32[]{:T(128)} %constant.175.clone.1, s32[]{:T(128)} %constant.185.clone.1) | dynamic-update-slice | bytes 6148 | tf_op jit(solution)/shard_map/scatter-add | solution.py:252
  102.7 2.7 collective-permute-start.5
  107.0 1.6 collective-permute-start.6
  108.6 2.2 collective-permute-start.7
  114.8 1.6 copy-done.7
  116.9 2.2 slice.642
  119.1 3.9 slice_add_fusion.7
  123.8 2.9 fusion.52
  126.7 3.0 copy.492
  129.7 5.6 %copy.591 = f32[3,16,16,128]{2,3,1,0:T(8,128)} copy(f32[3,16,16,128]{1,3,2,0:T(8,128)} %fusion.52) | data formatting | bytes 786432 | tf_op jit(solution)/shard_map/reshape | solution.py:116
  135.4 7.0 %fusion.38 = f32[3,16,16,128]{3,2,1,0:T(8,128)S(1)} fusion(f32[3,16,16,128]{2,3,1,0:T(8,128)} %copy.591, f32[128,128,1,1]{1,0,2,3:T(8,128)} %reshape.854), kind=kOutput, calls=%fused_computation.161 | convolution fusion | flops 150994944 | bytes 851968 | tf_op jit(solution)/shard_map/cxzb,ab->cxza/dot_general | solution.py:172
  142.5 3.6 fusion.14
  146.1 4.1 %fusion.20 = f32[3,16,16,128]{3,1,2,0:T(8,128)S(1)} fusion(f32[16,16,1,1]{1,0,3,2:T(8,128)S(1)} %copy-done.32, f32[3,16,16,128]{3,2,1,0:T(8,128)S(1)} %fusion.38, f32[3,16,16,128]{3,2,1,0:T(8,128)S(1)} %fusion.14, f32[3,16,16,128]{3,1,2,0:T(8,128)S(1)} %copy-done.18, f32[128]{0:T(128)S(1)} %copy-done.34, f32[16]{0:T(128)S(1)} %copy-done.40, ...), kind=kOutput, calls=%fused_computation.101 | convolution fusion | flops 19857408 | bytes 2099776 | tf_op jit(solution)/shard_map/ab,cbzy->cazy/dot_general | solution.py:170
  150.3 2.6 collective-permute-start.9
  152.9 1.6 collective-permute-done.8
  155.7 2.7 collective-permute-start.11
  158.4 1.9 collective-permute-done.10
  161.9 3.2 copy.509
  165.2 3.2 fusion.56
  168.5 2.5 slice.663
  171.0 5.1 %slice_add_fusion.5 = (f32[3,16,16,16,1]{1,4,3,2,0:T(1,128)S(1)}, f32[3,16,16,16,1]{1,4,3,2,0:T(1,128)S(1)}) fusion(f32[3,16,16,16,8]{1,4,3,2,0:T(8,128)} %bitcast.365, f32[3,16,16,15,1]{1,4,3,2,0:T(1,128)S(1)} %get-tuple-element.616, f32[3,16,16,15,1]{1,4,3,2,0:T(1,128)S(1)} %get-tuple-element.617), kind=kLoop, calls=%fused_computation.121 | loop fusion | flops 24576 | bytes 288768 | tf_op jit(solution)/shard_map/add | solution.py:115
  176.1 4.2 %multiply_reduce_fusion.6 = (f32[3]{0:T(128)}, f32[3]{0:T(128)}) fusion(f32[16,16,16,8]{0,3,2,1:T(8,128)S(1)} %copy-done.13, f32[3,16,16,16,1]{1,4,3,2,0:T(1,128)S(1)} %get-tuple-element.615, f32[3,16,16,16,6]{1,4,3,2,0:T(8,128)S(1)} %slice.663, f32[3,16,16,16,1]{1,4,3,2,0:T(1,128)S(1)} %get-tuple-element.614, f32[3,16,16,16,1]{1,4,3,2,0:T(1,128)S(1)} %copy-done.10, ...), kind=kLoop, calls=%fused_computation.85 | loop fusion | flops 983034 | bytes 917528 | tf_op jit(solution)/shard_map/reduce_sum | solution.py:185
  180.4 39.5 %all-reduce.12 = (f32[3]{0:T(128)}, f32[3]{0:T(128)}) all-reduce(f32[3]{0:T(128)} %get-tuple-element.523, f32[3]{0:T(128)} %get-tuple-element.522), channel_id=1, replica_groups=mesh['wall'=8,'span'=4] {'wall','span'}, use_global_device_ids=true, to_apply=%region_22.23 | all-reduce | flops 6 | bytes 48 | tf_op jit(solution)/shard_map/psum | solution.py:128
  220.6 6.0 %multiply_subtract_fusion.1 = (f32[3,16,16,16,8]{1,4,3,2,0:T(8,128)}, f32[3,16,16,128]{1,3,2,0:T(8,128)}) fusion(f32[3]{0:T(128)S(1)} %div.49, f32[3,16,16,16,1]{1,4,3,2,0:T(1,128)} %copy-done.17, f32[3,16,16,16,6]{1,4,3,2,0:T(8,128)} %copy-done, f32[3,16,16,16,1]{1,4,3,2,0:T(1,128)} %copy-done.16, f32[3,16,16,16,1]{1,4,3,2,0:T(1,128)} %copy-done.8, ...), kind=kLoop, calls=%fused_computation.84 | loop fusion | flops 589824 | bytes 1572876 | tf_op jit(solution)/shard_map/sub | solution.py:263
  226.5 3.2 copy.512
  231.4 2.1 fusion.12
  233.6 4.1 %copy.595 = f32[3,16,16,128]{2,3,1,0:T(8,128)} copy(f32[3,16,16,128]{1,3,2,0:T(8,128)S(1)} %bitcast.357) | data formatting | bytes 786432 | tf_op jit(solution)/shard_map/sub | solution.py:263
  237.6 7.0 %fusion.36 = f32[3,16,16,128]{3,2,1,0:T(8,128)S(1)} fusion(f32[3,16,16,128]{2,3,1,0:T(8,128)} %copy.595, f32[128,128,1,1]{1,0,2,3:T(8,128)} %reshape.854), kind=kOutput, calls=%fused_computation.159 | convolution fusion | flops 150994944 | bytes 851968 | tf_op jit(solution)/shard_map/cxzb,ab->cxza/dot_general | solution.py:172
  245.1 2.6 collective-permute-start.13
  247.7 1.5 collective-permute-done.12
  249.2 2.0 collective-permute-start.14
  251.2 1.9 collective-permute-start.15
  253.1 2.0 collective-permute-done.14
  257.8 2.1 copy.529
  261.7 2.0 copy-done.3
  264.0 3.0 multiply_reduce_fusion.4
  266.9 38.9 %all-reduce.11 = (f32[3]{0:T(128)}, f32[3]{0:T(128)}) all-reduce(f32[3]{0:T(128)} %get-tuple-element.527, f32[3]{0:T(128)} %get-tuple-element.526), channel_id=1, replica_groups=mesh['wall'=8,'span'=4] {'wall','span'}, use_global_device_ids=true, to_apply=%region_26.27 | all-reduce | flops 6 | bytes 48 | tf_op jit(solution)/shard_map/psum | solution.py:128
  307.1 6.7 %multiply_subtract_fusion = (f32[3,16,16,16,8]{1,4,3,2,0:T(8,128)}, f32[3,16,16,128]{1,3,2,0:T(8,128)}) fusion(f32[3,16,16,16,8]{1,4,3,2,0:T(8,128)} %get-tuple-element.604, f32[3]{0:T(128)S(1)} %get-tuple-element.570, f32[3]{0:T(128)S(1)} %get-tuple-element.568, f32[3,16,16,16,1]{1,4,3,2,0:T(1,128)} %copy-done.20, f32[3,16,16,16,6]{1,4,3,2,0:T(8,128)} %copy-done.6, ...), kind=kLoop, calls=%fused_computation.81 | loop fusion | flops 786432 | bytes 1966104 | tf_op jit(solution)/shard_map/sub | solution.py:263
  313.8 3.2 copy.533
  318.2 2.1 convolution_multiply_fusion
  321.7 4.1 %copy.596 = f32[3,16,16,128]{2,3,1,0:T(8,128)} copy(f32[3,16,16,128]{1,3,2,0:T(8,128)S(1)} %bitcast.358) | data formatting | bytes 786432 | tf_op jit(solution)/shard_map/sub | solution.py:263
  325.8 7.0 %fusion.34 = f32[3,16,16,128]{3,2,1,0:T(8,128)S(1)} fusion(f32[3,16,16,128]{2,3,1,0:T(8,128)} %copy.596, f32[128,128,1,1]{1,0,2,3:T(8,128)} %reshape.854), kind=kOutput, calls=%fused_computation.157 | convolution fusion | flops 150994944 | bytes 851968 | tf_op jit(solution)/shard_map/cxzb,ab->cxza/dot_general | solution.py:172
  333.4 2.6 collective-permute-start.17
  336.0 1.5 collective-permute-done.16
  337.5 2.1 collective-permute-start.18
  339.6 1.8 collective-permute-start.19
  346.1 3.3 copy.549
  349.4 3.2 fusion.54
  352.6 2.3 slice.705
  354.9 3.9 slice_add_fusion.1
  358.9 3.1 fusion.9
  362.0 39.9 %all-reduce.10 = (f32[3]{0:T(128)S(1)}, f32[3]{0:T(128)S(1)}) all-reduce(f32[3]{0:T(128)} %get-tuple-element.525, f32[3]{0:T(128)} %get-tuple-element.524), channel_id=1, replica_groups=mesh['wall'=8,'span'=4] {'wall','span'}, use_global_device_ids=true, to_apply=%region_30.31 | all-reduce | flops 6 | bytes 48 | tf_op jit(solution)/shard_map/psum | solution.py:128
  (760 shorter events, 91.2 us)
Async XLA Ops:
  7.2 44.4 %collective-permute-start.2 = (f32[4,128]{0,1:T(8,128)S(1)}, f32[4,128]{0,1:T(8,128)S(1)}, u32[]{:S(2)}, u32[]{:S(2)}) collective-permute-start(f32[4,128]{0,1:T(8,128)S(1)} %slice.614), channel_id=1, source_target_pairs={{0,28},{4,0},{8,4},{12,8},{16,12},{20,16},{24,20},{28,24},{1,29},{... | collective-permute-start | bytes 6152 | tf_op jit(solution)/shard_map/ppermute | solution.py:61
  12.9 39.0 %collective-permute-start = (f32[4,128]{0,1:T(8,128)S(1)}, f32[4,128]{0,1:T(8,128)S(1)}, u32[]{:S(2)}, u32[]{:S(2)}) collective-permute-start(f32[4,128]{0,1:T(8,128)S(1)} %slice.611), channel_id=1, source_target_pairs={{0,4},{4,8},{8,12},{12,16},{16,20},{20,24},{24,28},{28,0},{1,5},{5... | collective-permute-start | bytes 6152 | tf_op jit(solution)/shard_map/ppermute | solution.py:61
  14.6 6.8 %copy-start.33 = (f32[128]{0:T(128)}, f32[128]{0:T(128)S(1)}, u32[]{:S(2)}) copy-start(f32[128]{0:T(128)S(1)} %mul.576) | copy-start | bytes 1540
  15.4 5.9 %copy-start.39 = (f32[16]{0:T(128)S(1)}, f32[16]{0:T(128)}, u32[]{:S(2)}) copy-start(f32[16]{0:T(128)} %constant.191.clone) | copy-start | bytes 196
  15.4 5.9 %copy-start.48 = (f32[16]{0:T(128)S(1)}, f32[16]{0:T(128)}, u32[]{:S(2)}) copy-start(f32[16]{0:T(128)} %constant.190.clone) | copy-start | bytes 196
  15.4 6.1 %copy-start.25 = (f32[3,16,16,128]{3,2,1,0:T(8,128)S(1)}, f32[3,16,16,128]{3,2,1,0:T(8,128)}, u32[]{:S(2)}) copy-start(f32[3,16,16,128]{3,2,1,0:T(8,128)} %param.50) | copy-start | bytes 1179652
  21.5 6.9 %copy-start.21 = (f32[16,16,128]{2,0,1:T(8,128)}, f32[16,16,128]{2,0,1:T(8,128)S(1)}, u32[]{:S(2)}) copy-start(f32[16,16,128]{2,0,1:T(8,128)S(1)} %multiply_multiply_fusion) | copy-start | bytes 393220
  28.4 4.3 %copy-start.31 = (f32[8]{0:T(128)S(1)}, f32[8]{0:T(128)}, u32[]{:S(2)}) copy-start(f32[8]{0:T(128)} %constant.483) | copy-start | bytes 100
  32.7 18.7 %copy-start.51 = (f32[8,8]{1,0:T(8,128)S(1)}, f32[8,8]{1,0:T(8,128)}, u32[]{:S(2)}) copy-start(f32[8,8]{1,0:T(8,128)} %constant.189.clone) | copy-start | bytes 772
  67.9 23.6 %copy-start.52 = (f32[512]{0:T(512)S(1)}, f32[512]{0:T(512)}, u32[]{:S(2)}) copy-start(f32[512]{0:T(512)} %param.55) | copy-start | bytes 6148
  83.7 6.0 %collective-permute-start.3 = (f32[3,128]{0,1:T(8,128)S(1)}, f32[3,128]{0,1:T(8,128)S(1)}, u32[]{:S(2)}, u32[]{:S(2)}) collective-permute-start(f32[3,128]{0,1:T(8,128)S(1)} %bitcast.404), channel_id=1, source_target_pairs={{0,4},{4,8},{8,12},{12,16},{16,20},{20,24},{24,28},{28,0},{1,5},{5... | collective-permute-start | bytes 4616 | tf_op jit(solution)/shard_map/ppermute | solution.py:61
  83.7 4.8 %collective-permute-start.1 = (f32[3,128]{0,1:T(8,128)S(1)}, f32[3,128]{0,1:T(8,128)S(1)}, u32[]{:S(2)}, u32[]{:S(2)}) collective-permute-start(f32[3,128]{0,1:T(8,128)S(1)} %bitcast.405), channel_id=1, source_target_pairs={{0,28},{4,0},{8,4},{12,8},{16,12},{20,16},{24,20},{28,24},{1,29},{... | collective-permute-start | bytes 4616 | tf_op jit(solution)/shard_map/ppermute | solution.py:61
  102.6 4.3 %collective-permute-start.4 = (f32[3,1,16,128]{3,1,2,0:T(1,128)S(1)}, f32[3,1,16,128]{3,1,2,0:T(1,128)S(1)}, u32[]{:S(2)}, u32[]{:S(2)}) collective-permute-start(f32[3,1,16,128]{3,1,2,0:T(1,128)S(1)} %get-tuple-element.684), channel_id=1, source_target_pairs={{0,4},{4,8},{8,12},{12,16},{16,20},{20,24},{24,28},{28,0},{1,5},{5... | collective-permute-start | bytes 73736 | tf_op jit(solution)/shard_map/ppermute | solution.py:49
  102.7 4.3 %collective-permute-start.5 = (f32[3,1,16,128]{3,1,2,0:T(1,128)S(1)}, f32[3,1,16,128]{3,1,2,0:T(1,128)S(1)}, u32[]{:S(2)}, u32[]{:S(2)}) collective-permute-start(f32[3,1,16,128]{3,1,2,0:T(1,128)S(1)} %get-tuple-element.685), channel_id=1, source_target_pairs={{4,0},{8,4},{12,8},{16,12},{20,16},{24,20},{28,24},{0,28},{5,1},{9... | collective-permute-start | bytes 73736 | tf_op jit(solution)/shard_map/ppermute | solution.py:51
  107.0 5.9 %collective-permute-start.6 = (f32[3,18,1,128]{3,1,2,0:T(8,128)S(1)}, f32[3,18,1,128]{3,1,2,0:T(8,128)S(1)}, u32[]{:S(2)}, u32[]{:S(2)}) collective-permute-start(f32[3,18,1,128]{3,1,2,0:T(8,128)S(1)} %get-tuple-element.660), channel_id=1, source_target_pairs={{0,1},{1,2},{2,3},{3,0},{4,5},{5,6},{6,7},{7,4},{8,9},{9,10},{10,1... | collective-permute-start | bytes 82952 | tf_op jit(solution)/shard_map/ppermute | solution.py:49
  108.6 4.4 %collective-permute-start.7 = (f32[3,18,1,128]{3,1,2,0:T(8,128)S(1)}, f32[3,18,1,128]{3,1,2,0:T(8,128)S(1)}, u32[]{:S(2)}, u32[]{:S(2)}) collective-permute-start(f32[3,18,1,128]{3,1,2,0:T(8,128)S(1)} %get-tuple-element.661), channel_id=1, source_target_pairs={{1,0},{2,1},{3,2},{0,3},{5,4},{6,5},{7,6},{4,7},{9,8},{10,9},{11,1... | collective-permute-start | bytes 82952 | tf_op jit(solution)/shard_map/ppermute | solution.py:51
  135.3 7.1 %copy-start.4 = (f32[3,16,16,128]{2,3,1,0:T(8,128)S(1)}, f32[3,16,16,128]{2,3,1,0:T(8,128)}, u32[]{:S(2)}) copy-start(f32[3,16,16,128]{2,3,1,0:T(8,128)} %copy.591) | copy-start | bytes 1179652
  135.3 10.7 %copy-start.9 = (f32[3,16,16,16,1]{1,4,3,2,0:T(1,128)S(1)}, f32[3,16,16,16,1]{1,4,3,2,0:T(1,128)}, u32[]{:S(2)}) copy-start(f32[3,16,16,16,1]{1,4,3,2,0:T(1,128)} %copy-done.8) | copy-start | bytes 147460
  135.4 10.7 %copy-start.18 = (f32[3,16,16,128]{3,1,2,0:T(8,128)S(1)}, f32[3,16,16,128]{3,1,2,0:T(8,128)}, u32[]{:S(2)}) copy-start(f32[3,16,16,128]{3,1,2,0:T(8,128)} %copy.492) | copy-start | bytes 1179652
  135.4 10.7 %copy-start.22 = (f32[16,16,128]{2,0,1:T(8,128)S(1)}, f32[16,16,128]{2,0,1:T(8,128)}, u32[]{:S(2)}) copy-start(f32[16,16,128]{2,0,1:T(8,128)} %copy-done.21) | copy-start | bytes 393220
  135.4 10.7 %copy-start.32 = (f32[16,16,1,1]{1,0,3,2:T(8,128)S(1)}, f32[16,16,1,1]{1,0,3,2:T(8,128)}, u32[]{:S(2)}) copy-start(f32[16,16,1,1]{1,0,3,2:T(8,128)} %constant.242) | copy-start | bytes 3076
  135.4 10.7 %copy-start.34 = (f32[128]{0:T(128)S(1)}, f32[128]{0:T(128)}, u32[]{:S(2)}) copy-start(f32[128]{0:T(128)} %copy-done.33) | copy-start | bytes 1540
  135.4 10.7 %copy-start.40 = (f32[16]{0:T(128)S(1)}, f32[16]{0:T(128)}, u32[]{:S(2)}) copy-start(f32[16]{0:T(128)} %constant.191.clone) | copy-start | bytes 196
  150.2 4.3 %collective-permute-start.8 = (f32[3,1,16,128]{3,1,2,0:T(1,128)S(1)}, f32[3,1,16,128]{3,1,2,0:T(1,128)S(1)}, u32[]{:S(2)}, u32[]{:S(2)}) collective-permute-start(f32[3,1,16,128]{3,1,2,0:T(1,128)S(1)} %get-tuple-element.678), channel_id=1, source_target_pairs={{0,4},{4,8},{8,12},{12,16},{16,20},{20,24},{24,28},{28,0},{1,5},{5... | collective-permute-start | bytes 73736 | tf_op jit(solution)/shard_map/ppermute | solution.py:49
  150.3 4.2 %collective-permute-start.9 = (f32[3,1,16,128]{3,1,2,0:T(1,128)S(1)}, f32[3,1,16,128]{3,1,2,0:T(1,128)S(1)}, u32[]{:S(2)}, u32[]{:S(2)}) collective-permute-start(f32[3,1,16,128]{3,1,2,0:T(1,128)S(1)} %get-tuple-element.679), channel_id=1, source_target_pairs={{4,0},{8,4},{12,8},{16,12},{20,16},{24,20},{28,24},{0,28},{5,1},{9... | collective-permute-start | bytes 73736 | tf_op jit(solution)/shard_map/ppermute | solution.py:51
  154.5 5.8 %collective-permute-start.10 = (f32[3,18,1,128]{3,1,2,0:T(8,128)S(1)}, f32[3,18,1,128]{3,1,2,0:T(8,128)S(1)}, u32[]{:S(2)}, u32[]{:S(2)}) collective-permute-start(f32[3,18,1,128]{3,1,2,0:T(8,128)S(1)} %get-tuple-element.652), channel_id=1, source_target_pairs={{0,1},{1,2},{2,3},{3,0},{4,5},{5,6},{6,7},{7,4},{8,9},{9,10},{10,1... | collective-permute-start | bytes 82952 | tf_op jit(solution)/shard_map/ppermute | solution.py:49
  155.7 4.6 %collective-permute-start.11 = (f32[3,18,1,128]{3,1,2,0:T(8,128)S(1)}, f32[3,18,1,128]{3,1,2,0:T(8,128)S(1)}, u32[]{:S(2)}, u32[]{:S(2)}) collective-permute-start(f32[3,18,1,128]{3,1,2,0:T(8,128)S(1)} %get-tuple-element.653), channel_id=1, source_target_pairs={{1,0},{2,1},{3,2},{0,3},{5,4},{6,5},{7,6},{4,7},{9,8},{10,9},{11,1... | collective-permute-start | bytes 82952 | tf_op jit(solution)/shard_map/ppermute | solution.py:51
  168.4 7.7 %copy-start.10 = (f32[3,16,16,16,1]{1,4,3,2,0:T(1,128)S(1)}, f32[3,16,16,16,1]{1,4,3,2,0:T(1,128)}, u32[]{:S(2)}) copy-start(f32[3,16,16,16,1]{1,4,3,2,0:T(1,128)} %copy-done.8) | copy-start | bytes 147460
  168.4 7.7 %copy-start.13 = (f32[16,16,16,8]{0,3,2,1:T(8,128)S(1)}, f32[16,16,16,8]{0,3,2,1:T(8,128)}, u32[]{:S(2)}) copy-start(f32[16,16,16,8]{0,3,2,1:T(8,128)} %constant.217) | copy-start | bytes 393220
  171.0 9.4 %copy-start = (f32[3,16,16,16,6]{1,4,3,2,0:T(8,128)}, f32[3,16,16,16,6]{1,4,3,2,0:T(8,128)S(1)}, u32[]{:S(2)}) copy-start(f32[3,16,16,16,6]{1,4,3,2,0:T(8,128)S(1)} %slice.663) | copy-start | bytes 884740
  176.1 4.3 %copy-start.16 = (f32[3,16,16,16,1]{1,4,3,2,0:T(1,128)}, f32[3,16,16,16,1]{1,4,3,2,0:T(1,128)S(1)}, u32[]{:S(2)}) copy-start(f32[3,16,16,16,1]{1,4,3,2,0:T(1,128)S(1)} %get-tuple-element.614) | copy-start | bytes 147460
  176.1 4.3 %copy-start.17 = (f32[3,16,16,16,1]{1,4,3,2,0:T(1,128)}, f32[3,16,16,16,1]{1,4,3,2,0:T(1,128)S(1)}, u32[]{:S(2)}) copy-start(f32[3,16,16,16,1]{1,4,3,2,0:T(1,128)S(1)} %get-tuple-element.615) | copy-start | bytes 147460
  220.6 6.0 %copy-start.49 = (f32[3]{0:T(128)}, f32[3]{0:T(128)S(1)}, u32[]{:S(2)}) copy-start(f32[3]{0:T(128)S(1)} %div.49) | copy-start | bytes 40
  226.5 7.0 %copy-start.2 = (f32[3,16,16,16,8]{1,4,3,2,0:T(8,128)S(1)}, f32[3,16,16,16,8]{1,4,3,2,0:T(8,128)}, u32[]{:S(2)}) copy-start(f32[3,16,16,16,8]{1,4,3,2,0:T(8,128)} %get-tuple-element.604) | copy-start | bytes 1179652
  237.6 7.0 %copy-start.23 = (f32[16,16,128]{2,0,1:T(8,128)S(1)}, f32[16,16,128]{2,0,1:T(8,128)}, u32[]{:S(2)}) copy-start(f32[16,16,128]{2,0,1:T(8,128)} %copy-done.21) | copy-start | bytes 393220
  237.6 7.0 %copy-start.28 = (f32[3,16,16,128]{3,2,1,0:T(8,128)S(1)}, f32[3,16,16,128]{3,2,1,0:T(8,128)}, u32[]{:S(2)}) copy-start(f32[3,16,16,128]{3,2,1,0:T(8,128)} %fusion.12) | copy-start | bytes 1179652
  245.0 4.2 %collective-permute-start.12 = (f32[3,1,16,128]{3,1,2,0:T(1,128)S(1)}, f32[3,1,16,128]{3,1,2,0:T(1,128)S(1)}, u32[]{:S(2)}, u32[]{:S(2)}) collective-permute-start(f32[3,1,16,128]{3,1,2,0:T(1,128)S(1)} %get-tuple-element.672), channel_id=1, source_target_pairs={{0,4},{4,8},{8,12},{12,16},{16,20},{20,24},{24,28},{28,0},{1,5},{5... | collective-permute-start | bytes 73736 | tf_op jit(solution)/shard_map/ppermute | solution.py:49
  245.1 4.2 %collective-permute-start.13 = (f32[3,1,16,128]{3,1,2,0:T(1,128)S(1)}, f32[3,1,16,128]{3,1,2,0:T(1,128)S(1)}, u32[]{:S(2)}, u32[]{:S(2)}) collective-permute-start(f32[3,1,16,128]{3,1,2,0:T(1,128)S(1)} %get-tuple-element.673), channel_id=1, source_target_pairs={{4,0},{8,4},{12,8},{16,12},{20,16},{24,20},{28,24},{0,28},{5,1},{9... | collective-permute-start | bytes 73736 | tf_op jit(solution)/shard_map/ppermute | solution.py:51
  249.2 5.8 %collective-permute-start.14 = (f32[3,18,1,128]{3,1,2,0:T(8,128)S(1)}, f32[3,18,1,128]{3,1,2,0:T(8,128)S(1)}, u32[]{:S(2)}, u32[]{:S(2)}) collective-permute-start(f32[3,18,1,128]{3,1,2,0:T(8,128)S(1)} %get-tuple-element.644), channel_id=1, source_target_pairs={{0,1},{1,2},{2,3},{3,0},{4,5},{5,6},{6,7},{7,4},{8,9},{9,10},{10,1... | collective-permute-start | bytes 82952 | tf_op jit(solution)/shard_map/ppermute | solution.py:49
  251.2 5.0 %collective-permute-start.15 = (f32[3,18,1,128]{3,1,2,0:T(8,128)S(1)}, f32[3,18,1,128]{3,1,2,0:T(8,128)S(1)}, u32[]{:S(2)}, u32[]{:S(2)}) collective-permute-start(f32[3,18,1,128]{3,1,2,0:T(8,128)S(1)} %get-tuple-element.645), channel_id=1, source_target_pairs={{1,0},{2,1},{3,2},{0,3},{5,4},{6,5},{7,6},{4,7},{9,8},{10,9},{11,1... | collective-permute-start | bytes 82952 | tf_op jit(solution)/shard_map/ppermute | solution.py:51
  260.7 6.2 %copy-start.6 = (f32[3,16,16,16,6]{1,4,3,2,0:T(8,128)}, f32[3,16,16,16,6]{1,4,3,2,0:T(8,128)S(1)}, u32[]{:S(2)}) copy-start(f32[3,16,16,16,6]{1,4,3,2,0:T(8,128)S(1)} %slice.684) | copy-start | bytes 884740
  261.7 5.3 %copy-start.19 = (f32[3,16,16,16,1]{1,4,3,2,0:T(1,128)}, f32[3,16,16,16,1]{1,4,3,2,0:T(1,128)S(1)}, u32[]{:S(2)}) copy-start(f32[3,16,16,16,1]{1,4,3,2,0:T(1,128)S(1)} %get-tuple-element.610) | copy-start | bytes 147460
  261.7 5.3 %copy-start.20 = (f32[3,16,16,16,1]{1,4,3,2,0:T(1,128)}, f32[3,16,16,16,1]{1,4,3,2,0:T(1,128)S(1)}, u32[]{:S(2)}) copy-start(f32[3,16,16,16,1]{1,4,3,2,0:T(1,128)S(1)} %get-tuple-element.611) | copy-start | bytes 147460
  264.0 43.1 %copy-start.1 = (f32[3,16,16,16,6]{1,4,3,2,0:T(8,128)S(1)}, f32[3,16,16,16,6]{1,4,3,2,0:T(8,128)}, u32[]{:S(2)}) copy-start(f32[3,16,16,16,6]{1,4,3,2,0:T(8,128)} %copy-done) | copy-start | bytes 884740
  307.1 6.7 %copy-start.42 = (f32[3]{0:T(128)}, f32[3]{0:T(128)S(1)}, u32[]{:S(2)}) copy-start(f32[3]{0:T(128)S(1)} %get-tuple-element.568) | copy-start | bytes 40
  307.1 6.7 %copy-start.44 = (f32[3]{0:T(128)}, f32[3]{0:T(128)S(1)}, u32[]{:S(2)}) copy-start(f32[3]{0:T(128)S(1)} %get-tuple-element.570) | copy-start | bytes 40
  313.8 7.9 %copy-start.5 = (f32[3,16,16,16,8]{1,4,3,2,0:T(8,128)S(1)}, f32[3,16,16,16,8]{1,4,3,2,0:T(8,128)}, u32[]{:S(2)}) copy-start(f32[3,16,16,16,8]{1,4,3,2,0:T(8,128)} %get-tuple-element.602) | copy-start | bytes 1179652
  325.8 7.0 %copy-start.12 = (f32[3,16,16,128]{3,1,2,0:T(8,128)S(1)}, f32[3,16,16,128]{3,1,2,0:T(8,128)}, u32[]{:S(2)}) copy-start(f32[3,16,16,128]{3,1,2,0:T(8,128)} %copy-done.11) | copy-start | bytes 1179652
  325.8 7.1 %copy-start.24 = (f32[16,16,128]{2,0,1:T(8,128)S(1)}, f32[16,16,128]{2,0,1:T(8,128)}, u32[]{:S(2)}) copy-start(f32[16,16,128]{2,0,1:T(8,128)} %copy-done.21) | copy-start | bytes 393220
  325.8 7.1 %copy-start.26 = (f32[3,16,128,16]{2,3,1,0:T(8,128)S(1)}, f32[3,16,128,16]{2,3,1,0:T(8,128)}, u32[]{:S(2)}) copy-start(f32[3,16,128,16]{2,3,1,0:T(8,128)} %convolution_multiply_fusion) | copy-start | bytes 1179652
  325.8 7.1 %copy-start.27 = (f32[3,16,16,128]{3,2,1,0:T(8,128)S(1)}, f32[3,16,16,128]{3,2,1,0:T(8,128)}, u32[]{:S(2)}) copy-start(f32[3,16,16,128]{3,2,1,0:T(8,128)} %fusion.27) | copy-start | bytes 1179652
  325.8 7.1 %copy-start.36 = (f32[128]{0:T(128)S(1)}, f32[128]{0:T(128)}, u32[]{:S(2)}) copy-start(f32[128]{0:T(128)} %copy-done.33) | copy-start | bytes 1540
  325.8 15.6 %copy-start.38 = (f32[512]{0:T(512)S(1)}, f32[512]{0:T(512)}, u32[]{:S(2)}) copy-start(f32[512]{0:T(512)} %copy-done.37) | copy-start | bytes 6148
  325.8 15.6 %copy-start.46 = (f32[1,512]{1,0:T(1,128)S(1)}, f32[1,512]{1,0:T(1,128)}, u32[]{:S(2)}) copy-start(f32[1,512]{1,0:T(1,128)} %get-tuple-element.690) | copy-start | bytes 6148
  325.8 15.6 %copy-start.47 = (f32[1,512]{1,0:T(1,128)S(1)}, f32[1,512]{1,0:T(1,128)}, u32[]{:S(2)}) copy-start(f32[1,512]{1,0:T(1,128)} %get-tuple-element.694) | copy-start | bytes 6148
  333.3 4.2 %collective-permute-start.16 = (f32[3,1,16,128]{3,1,2,0:T(1,128)S(1)}, f32[3,1,16,128]{3,1,2,0:T(1,128)S(1)}, u32[]{:S(2)}, u32[]{:S(2)}) collective-permute-start(f32[3,1,16,128]{3,1,2,0:T(1,128)S(1)} %get-tuple-element.666), channel_id=1, source_target_pairs={{0,4},{4,8},{8,12},{12,16},{16,20},{20,24},{24,28},{28,0},{1,5},{5... | collective-permute-start | bytes 73736 | tf_op jit(solution)/shard_map/ppermute | solution.py:49
  333.4 4.2 %collective-permute-start.17 = (f32[3,1,16,128]{3,1,2,0:T(1,128)S(1)}, f32[3,1,16,128]{3,1,2,0:T(1,128)S(1)}, u32[]{:S(2)}, u32[]{:S(2)}) collective-permute-start(f32[3,1,16,128]{3,1,2,0:T(1,128)S(1)} %get-tuple-element.667), channel_id=1, source_target_pairs={{4,0},{8,4},{12,8},{16,12},{20,16},{24,20},{28,24},{0,28},{5,1},{9... | collective-permute-start | bytes 73736 | tf_op jit(solution)/shard_map/ppermute | solution.py:51
  337.5 5.8 %collective-permute-start.18 = (f32[3,18,1,128]{3,1,2,0:T(8,128)S(1)}, f32[3,18,1,128]{3,1,2,0:T(8,128)S(1)}, u32[]{:S(2)}, u32[]{:S(2)}) collective-permute-start(f32[3,18,1,128]{3,1,2,0:T(8,128)S(1)} %get-tuple-element.636), channel_id=1, source_target_pairs={{0,1},{1,2},{2,3},{3,0},{4,5},{5,6},{6,7},{7,4},{8,9},{9,10},{10,1... | collective-permute-start | bytes 82952 | tf_op jit(solution)/shard_map/ppermute | solution.py:49
  339.6 4.8 %collective-permute-start.19 = (f32[3,18,1,128]{3,1,2,0:T(8,128)S(1)}, f32[3,18,1,128]{3,1,2,0:T(8,128)S(1)}, u32[]{:S(2)}, u32[]{:S(2)}) collective-permute-start(f32[3,18,1,128]{3,1,2,0:T(8,128)S(1)} %get-tuple-element.637), channel_id=1, source_target_pairs={{1,0},{2,1},{3,2},{0,3},{5,4},{6,5},{7,6},{4,7},{9,8},{10,9},{11,1... | collective-permute-start | bytes 82952 | tf_op jit(solution)/shard_map/ppermute | solution.py:51
  352.6 6.3 %copy-start.15 = (f32[16,16,16,8]{0,3,2,1:T(8,128)S(1)}, f32[16,16,16,8]{0,3,2,1:T(8,128)}, u32[]{:S(2)}) copy-start(f32[16,16,16,8]{0,3,2,1:T(8,128)} %constant.217) | copy-start | bytes 393220
  358.9 43.0 %copy-start.53 = (f32[3]{0:T(128)S(1)}, f32[3]{0:T(128)}, u32[]{:S(2)}) copy-start(f32[3]{0:T(128)} %get-tuple-element.562) | copy-start | bytes 40
  358.9 43.6 %copy-start.43 = (f32[3]{0:T(128)S(1)}, f32[3]{0:T(128)}, u32[]{:S(2)}) copy-start(f32[3]{0:T(128)} %copy-done.42) | copy-start | bytes 40
  358.9 43.6 %copy-start.45 = (f32[3]{0:T(128)S(1)}, f32[3]{0:T(128)}, u32[]{:S(2)}) copy-start(f32[3]{0:T(128)} %copy-done.44) | copy-start | bytes 40
  358.9 43.6 %copy-start.50 = (f32[3]{0:T(128)S(1)}, f32[3]{0:T(128)}, u32[]{:S(2)}) copy-start(f32[3]{0:T(128)} %copy-done.49) | copy-start | bytes 40
  (10 other events, 28.1 us)
where the time goes:
time: 413 us; the launch traced here: 405 us
  local copies, waits for them, and re-layouts  126 us (31%)
  blocking collectives  118 us (29%)
  other arithmetic  73.3 us (18%)
  matrix products  33.8 us (8%)
  starting transfers between devices  32.8 us (8%)
  waiting for transfers between devices  16.1 us (4%)
    psum x3, blocking collectives, paired_total(): return lax.psum((first, second), ('wall', 'span'))  118 us
    dot_general x3, matrix products, operate(): along_y = jnp.einsum('cxzb,ab->cxza', field, stiff_y, precision=precise)  21 us
    ppermute x8, starting transfers between devices, with_halo(): lax.ppermute(head, axis, [((i + 1) % count, i) for i in range(count)])  19.2 us
    gather x24, local copies, waits for them, and re-layouts, evaluate(): values = element_rows[row_ids].reshape(row_ids.shape[0], 3, 8, 8, 8)  15.4 us
    sub x4, other arithmetic, body(): residual = residual - spread(step_size) * along_dir  15.1 us
    reshape x4, local copies, waits for them, and re-layouts, join_faces(): return joined.reshape(core.shape)  15 us
    add x12, other arithmetic, join_faces(): first + prev_last  14.2 us
    while x96, local copies, waits for them, and re-layouts  12.7 us
  transfers between devices with their start and end apart: 20, of which 13 were waited for; matrix products, arithmetic and copies ran while one was open for 11% of the time, Pallas kernels for 0%

commit v1 on v0

v1 whole, which is shorter than its diff:
```python
import functools

import jax
import jax.numpy as jnp
import numpy as np
from jax import lax
from jax.experimental import pallas as pl
from jax.experimental.pallas import tpu as pltpu
from jax.sharding import PartitionSpec as P

GLL_NODES = (
    -1.0,
    -0.8717401485096066,
    -0.5917001814331423,
    -0.2092992179024789,
    0.2092992179024789,
    0.5917001814331423,
    0.8717401485096066,
    1.0,
)
GLL_WEIGHTS = (
    0.03571428571428571,
    0.2107042271435061,
    0.3411226924835044,
    0.4124587946587038,
    0.4124587946587038,
    0.3411226924835044,
    0.2107042271435061,
    0.03571428571428571,
)
viscosity = 0.02
inverse_step = 20.0
karman = 0.41
sample_height = 0.1
speed_floor = 0.01
element_dx = 0.05
element_dz = 0.13
NEAR = 2
ROUNDS = 3
MESH = pl.DeviceIdType.MESH
F32 = jnp.float32
BF16 = jnp.bfloat16


def stiffness_table():
    points = np.array(GLL_NODES)
    weights = np.array(GLL_WEIGHTS)
    previous = np.ones(8)
    current = points.copy()
    for degree in range(1, 7):
        previous, current = (
            current,
            ((2 * degree + 1) * points * current - degree * previous) / (degree + 1),
        )
    derivative = np.zeros((8, 8))
    for target in range(8):
        for source in range(8):
            if target != source:
                derivative[target, source] = (
                    current[target] / current[source] / (points[target] - points[source])
                )
    derivative[0, 0] = -14.0
    derivative[7, 7] = 14.0
    return derivative.T @ (weights[:, None] * derivative)


def join_matrix(length):
    joined = np.eye(length)
    for left in range(7, length - 1, 8):
        joined[left, left + 1] = 1.0
        joined[left + 1, left] = 1.0
    return joined


def face_weights(length, open_ends):
    values = np.ones(length)
    position = np.arange(length) % 8
    values[(position == 0) | (position == 7)] = 0.5
    if open_ends:
        values[0] = 1.0
        values[-1] = 1.0
    return values


def split_np(matrix):
    single = jnp.asarray(matrix, F32)
    high = single.astype(BF16)
    low = (jnp.asarray(matrix, F32) - high.astype(F32)).astype(BF16)
    return high, low


def tables(length_x, length_z, length_y):
    weights = np.array(GLL_WEIGHTS)
    stiffness = stiffness_table()
    count_x, count_z, count_y = length_x // 8, length_z // 8, length_y // 8
    mass_x = np.tile(0.5 * element_dx * weights, count_x)
    mass_z = np.tile(0.5 * element_dz * weights, count_z)
    stiff_x = np.kron(np.eye(count_x), stiffness * (2.0 / element_dx))
    stiff_z = np.kron(np.eye(count_z), stiffness * (2.0 / element_dz))
    mass_xz = np.kron(mass_x, mass_z)
    join_xz = np.kron(join_matrix(length_x), join_matrix(length_z))
    join_y = join_matrix(length_y)
    plane = viscosity * (
        np.kron(stiff_x, np.diag(mass_z)) + np.kron(np.diag(mass_x), stiff_z)
    ) + inverse_step * np.diag(mass_xz)
    plane = join_xz @ plane
    mass_plane = join_xz @ np.diag(mass_xz)
    both = np.concatenate([plane, mass_plane], axis=1)
    lines_mass = np.tile(0.5 * weights, count_y)[:, None] * join_y
    lines_stiff = viscosity * 2.0 * (np.kron(np.eye(count_y), stiffness) @ join_y)
    lines = np.stack([lines_mass, lines_stiff])
    full = np.tile(mass_x, 3)
    ring_x = join_matrix(length_x) @ mass_x
    ring_z = join_matrix(length_z) @ mass_z
    ring_x[0] *= 2.0
    ring_x[-1] *= 2.0
    ring_z[0] *= 2.0
    ring_z[-1] *= 2.0
    del full
    assembled = inverse_step * np.kron(ring_x, ring_z)
    inner_x = face_weights(length_x, True)
    inner_z = face_weights(length_z, True)
    outer_x = face_weights(length_x, False)
    outer_z = face_weights(length_z, False)
    weight_y = face_weights(length_y, True)
    columns = np.stack(
        [
            assembled[:, None] * np.ones(length_y)[None],
            np.kron(outer_x, outer_z)[:, None] * weight_y[None],
            np.kron(inner_x, inner_z)[:, None] * weight_y[None],
        ]
    )
    return both, lines, columns


def split(value):
    high = value.astype(BF16)
    low = (value - high.astype(F32)).astype(BF16)
    return high, low


def dot3(left, right, dims):
    def one(a, b):
        return lax.dot_general(a, b, (dims, ((), ())), preferred_element_type=F32)

    return one(left[0], right[0]) + (one(left[0], right[1]) + one(left[1], right[0]))


NN = ((1,), (0,))
NT = ((1,), (1,))
TN = ((0,), (0,))
DIRS = ((1, 1), (1, -1), (-1, 1), (-1, -1))


def lagrange_rows(coord):
    points = np.array(GLL_NODES)
    scale = 1.0 / np.prod(points[:, None] - points[None, :] + np.eye(8), axis=1)
    shape = (8, coord.shape[1])
    node = lax.broadcasted_iota(jnp.int32, shape, 0)
    total = jnp.zeros(shape, F32)
    for a in range(8):
        total = jnp.where(node == a, F32(scale[a]), total)
    for b in range(8):
        total = total * jnp.where(node == b, F32(1.0), coord - F32(points[b]))
    return total


def kernel(
    n_wall,
    n_span,
    sizes,
    vel,
    heights,
    owner,
    element,
    coords,
    roughness,
    plane_hi,
    plane_lo,
    lines,
    columns,
    out,
    neumann,
    near,
    near_got,
    field,
    local,
    z_send,
    c_send,
    x_got,
    z_got,
    c_got,
    parts,
    sum_send,
    wall_got,
    span_got,
    near_ss,
    near_rs,
    face_ss,
    face_rs,
    wall_ss,
    wall_rs,
    span_ss,
    span_rs,
):
    length_x, length_z, length_y = sizes
    rows = length_x * length_z
    count_z, count_y = length_z // 8, length_y // 8
    w = lax.axis_index("wall")
    s = lax.axis_index("span")

    def at(dx, dz):
        return (lax.rem(w + (dx + n_wall), n_wall), lax.rem(s + (dz + n_span), n_span))

    greeted = [(k, 0) for k in range(1, n_wall)] + [(0, k) for k in range(1, n_span)]
    greeted += list(DIRS)
    barrier = pltpu.get_barrier_semaphore()
    for dx, dz in greeted:
        pl.semaphore_signal(barrier, inc=1, device_id=at(dx, dz), device_id_type=MESH)

    lane = lax.broadcasted_iota(jnp.int32, (64, length_y), 1)
    groups = (length_x // 8) * count_z
    for index, comp in enumerate((0, 2)):
        packed = jnp.zeros((64, length_y), F32)
        for group in range(groups):
            ex, ez = group // count_z, group % count_z
            block = vel[comp, pl.ds(ex * 8, 8), pl.ds(ez * 8, 8), :].reshape(64, length_y)
            moved = pltpu.roll(block, (group * 32 + 16) % length_y, 1)
            packed = jnp.where(lane // 32 == group, moved, packed)
        near[index] = packed
    pl.semaphore_wait(barrier, len(greeted))

    def remote(src, dst, ss, rs, where):
        return pltpu.make_async_remote_copy(
            src_ref=src,
            dst_ref=dst,
            send_sem=ss,
            recv_sem=rs,
            device_id=where,
            device_id_type=MESH,
        )

    near_copies = []
    for slot, dx in enumerate((1, -1)):
        copy = remote(near, near_got.at[slot], near_ss.at[slot], near_rs.at[slot], at(dx, 0))
        copy.start()
        near_copies.append(copy)

    layer_of = lax.broadcasted_iota(jnp.int32, (length_y, count_y), 0) // 8
    layer = lax.broadcasted_iota(jnp.int32, (length_y, count_y), 1)
    height_row = heights[...]
    height = jnp.sum(jnp.where(layer_of == layer, height_row, 0.0), axis=1, keepdims=True)
    lines_mass = height * lines[0]
    lines_hi, lines_lo = split(jnp.concatenate([lines_mass, lines[1] / height], axis=1))
    bound = jnp.max(0.1535 * height_row + 0.000182 / height_row, axis=1, keepdims=True)
    shifts = (0.15 * bound, 0.85 * bound)

    mass_row = jnp.sum(lines_mass, axis=0, keepdims=True)
    scale = columns[0] * mass_row
    for c in range(3):
        field[0, c] = vel[c].reshape(rows, length_y) * scale

    points = owner.shape[1]
    row_x = lagrange_rows(coords[0:1, :])
    row_z = lagrange_rows(coords[1:2, :])
    row_y = lagrange_rows(coords[2:3, :])
    cross = jnp.concatenate([row_x[a : a + 1] * row_z for a in range(8)], axis=0)
    distance = lax.rem(owner[...] - w + n_wall, n_wall)
    from_next = distance == 1
    from_prev = distance == n_wall - 1
    own = jnp.logical_not(jnp.logical_or(from_next, from_prev))
    spread = jnp.concatenate(
        [jnp.where(mask, cross, 0.0) for mask in (own, from_prev, from_next)], axis=0
    )
    n_row = lax.broadcasted_iota(jnp.int32, (length_y, points), 0)
    within = (n_row % 32) // 8
    layer_y = jnp.where(within < NEAR, within + (count_y - NEAR), within - NEAR)
    wanted = (n_row // 32) * count_y + layer_y == element[...]
    along = jnp.where(wanted, jnp.concatenate([row_y] * (length_y // 8), axis=0), 0.0)
    spread = split(spread)

    for copy in near_copies:
        copy.wait()

    sampled = []
    for index in range(2):
        sources = jnp.concatenate(
            [near[index], near_got[0, index], near_got[1, index]], axis=0
        )
        values = dot3(split(sources), spread, TN)
        sampled.append(jnp.sum(values * along, axis=0, keepdims=True))
    stream, spanwise = sampled
    speed = jnp.sqrt(stream * stream + spanwise * spanwise + speed_floor)
    drag = karman / jnp.log(sample_height / roughness[...])
    factor = -(drag * drag * speed / viscosity)
    gradient = (factor * stream, factor * spanwise)
    neumann[0:1, :] = gradient[0]
    neumann[1:2, :] = gradient[1]

    def face_copies(turn):
        copies = []
        for slot, dx in enumerate((1, -1)):
            start = rows - length_z if dx == 1 else 0
            copies.append(
                remote(
                    local.at[turn, :, pl.ds(start, length_z), :],
                    x_got.at[turn, slot],
                    face_ss.at[turn, slot],
                    face_rs.at[turn, slot],
                    at(dx, 0),
                )
            )
        for slot, dz in enumerate((1, -1)):
            copies.append(
                remote(
                    z_send.at[turn, slot],
                    z_got.at[turn, slot],
                    face_ss.at[turn, 2 + slot],
                    face_rs.at[turn, 2 + slot],
                    at(0, dz),
                )
            )
        for slot, (dx, dz) in enumerate(DIRS):
            copies.append(
                remote(
                    c_send.at[turn, slot],
                    c_got.at[turn, slot],
                    face_ss.at[turn, 4 + slot],
                    face_rs.at[turn, 4 + slot],
                    at(dx, dz),
                )
            )
        return copies

    def corner(dx, dz):
        return (rows - length_z if dx == 1 else 0) + (length_z - 1 if dz == 1 else 0)

    def send_faces(turn):
        for c in range(3):
            for slot, dz in enumerate((1, -1)):
                edge = length_z - 1 if dz == 1 else 0
                z_send[turn, slot, c] = local[turn, c, pl.ds(edge, length_x, stride=length_z), :]
            for slot, (dx, dz) in enumerate(DIRS):
                at_row = corner(dx, dz)
                c_send[turn, slot, c : c + 1, :] = local[turn, c, at_row : at_row + 1, :]
        for slot in range(4):
            c_send[turn, slot, 3:8, :] = jnp.zeros((5, length_y), F32)
        copies = face_copies(turn)
        for copy in copies:
            copy.start()
        return copies

    def add_faces(turn, copies):
        for copy in copies:
            copy.wait()
        for c in range(3):
            for slot, dx in enumerate((1, -1)):
                start = 0 if dx == 1 else rows - length_z
                field[turn, c, pl.ds(start, length_z), :] += x_got[turn, slot, c]
            for slot, dz in enumerate((1, -1)):
                edge = pl.ds(0 if dz == 1 else length_z - 1, length_x, stride=length_z)
                field[turn, c, edge, :] = field[turn, c, edge, :] + z_got[turn, slot, c]
            for slot, (dx, dz) in enumerate(DIRS):
                at_row = corner(-dx, -dz)
                field[turn, c, at_row : at_row + 1, :] += c_got[turn, slot, c : c + 1, :]

    def inner(quantity, c, product):
        parts[quantity * 8 + c : quantity * 8 + c + 1, :] = jnp.sum(
            product, axis=0, keepdims=True
        )

    n_line = lax.broadcasted_iota(jnp.int32, (length_y, rows), 0)
    mass_hi = plane_hi[:, rows:]
    mass_lo = plane_lo[:, rows:]
    for index, c in enumerate((0, 2)):
        pull = viscosity * gradient[index]
        lifted = jnp.where(
            n_line == 0, pull[:, :rows], jnp.where(n_line == length_y - 1, pull[:, rows:], 0.0)
        )
        local[0, c] = dot3((mass_hi, mass_lo), split(lifted), NT)
    local[0, 1] = jnp.zeros((rows, length_y), F32)
    copies = send_faces(0)
    parts[...] = jnp.zeros_like(parts)
    for c in (0, 2):
        field[0, c] += local[0, c]
    add_faces(0, copies)

    def operate(source, target):
        for c in range(3):
            lined = dot3(split(field[source, c]), (lines_hi, lines_lo), NN)
            stacked = jnp.concatenate([lined[:, :length_y], lined[:, length_y:]], axis=0)
            local[target, c] = dot3((plane_hi[...], plane_lo[...]), split(stacked), NN)

    slots = {(0, 0): 0, (0, 1): 1, (1, 1): 2, (0, 2): 3, (1, 2): 4, (2, 2): 5}

    def inner_products(newest):
        for c in range(3):
            weighted = field[newest, c] * columns[1]
            for other in range(newest + 1):
                inner(slots[(other, newest)], c, weighted * field[other, c])

    for turn in (1, 2):
        operate(turn - 1, turn)
        copies = send_faces(turn)
        for c in range(3):
            field[turn, c] = local[turn, c] - shifts[turn - 1] * field[turn - 1, c]
        inner_products(turn - 1)
        add_faces(turn, copies)
    operate(2, 3)
    inner_products(2)
    for c in range(3):
        inner(6, c, field[2, c] * columns[2] * local[3, c])

    total_rows = parts.shape[0]
    r_iota = lax.broadcasted_iota(jnp.int32, (total_rows, 128), 0)
    l_iota = lax.broadcasted_iota(jnp.int32, (total_rows, 128), 1)
    diagonal = r_iota == l_iota
    summed = jnp.sum(parts[...], axis=1, keepdims=True)
    row = jnp.sum(jnp.where(diagonal, summed, 0.0), axis=0, keepdims=True)

    def gather_sum(stage, row, count, got, ss, rs, place):
        sum_send[stage] = jnp.broadcast_to(row, (8, 128))
        copies = []
        for k in range(1, count):
            copy = remote(
                sum_send.at[stage], got.at[k - 1], ss.at[k - 1], rs.at[k - 1], place(k)
            )
            copy.start()
            copies.append(copy)
        for copy in copies:
            copy.wait()
        total = row
        for k in range(1, count):
            total = total + got[k - 1, 0:1, :]
        return total

    row = gather_sum(0, row, n_wall, wall_got, wall_ss, wall_rs, lambda k: at(k, 0))
    row = gather_sum(1, row, n_span, span_got, span_ss, span_rs, lambda k: at(0, k))
    totals = jnp.sum(jnp.where(diagonal, row, 0.0), axis=1, keepdims=True)
    m00, m01, m11, m02, m12, m22, e22 = [totals[q * 8 : q * 8 + 8, :] for q in range(7)]
    t1, t2 = shifts
    a00 = m01 + t1 * m00
    a01 = m11 + t1 * m01
    a02 = m12 + t1 * m02
    a11 = m12 + t2 * m11
    a12 = m22 + t2 * m12
    l10 = a01 / a00
    l20 = a02 / a00
    d1 = a11 - l10 * a01
    u12 = a12 - l10 * a02
    l21 = u12 / d1
    d2 = e22 - l20 * a02 - l21 * u12
    y1 = m01 - l10 * m00
    y2 = m02 - l20 * m00 - l21 * y1
    x2 = y2 / d2
    x1 = y1 / d1 - l21 * x2
    x0 = m00 / a00 - l10 * x1 - l20 * x2
    for c in range(3):
        result = (
            x0[c : c + 1] * field[0, c] + x1[c : c + 1] * field[1, c] + x2[c : c + 1] * field[2, c]
        )
        out[c] = result.reshape(length_x, length_z, length_y)


def body(n_wall, n_span, velocity_old, heights, owner_device, owner_element, ref_coords, roughness):
    sizes = velocity_old.shape[1:]
    length_x, length_z, length_y = sizes
    rows = length_x * length_z
    points = owner_device.shape[0]
    both, lines, columns = tables(*sizes)
    plane_hi, plane_lo = split_np(both)
    vmem = pl.BlockSpec(memory_space=pltpu.VMEM)
    dma = pltpu.SemaphoreType.DMA
    return pl.pallas_call(
        functools.partial(kernel, n_wall, n_span, sizes),
        out_shape=(
            jax.ShapeDtypeStruct(velocity_old.shape, F32),
            jax.ShapeDtypeStruct((2, points), F32),
        ),
        in_specs=[vmem] * 10,
        out_specs=(vmem, vmem),
        scratch_shapes=[
            pltpu.VMEM((2, 64, length_y), F32),
            pltpu.VMEM((2, 2, 64, length_y), F32),
            pltpu.VMEM((3, 3, rows, length_y), F32),
            pltpu.VMEM((4, 3, rows, length_y), F32),
            pltpu.VMEM((ROUNDS, 2, 3, length_x, length_y), F32),
            pltpu.VMEM((ROUNDS, 4, 8, length_y), F32),
            pltpu.VMEM((ROUNDS, 2, 3, length_z, length_y), F32),
            pltpu.VMEM((ROUNDS, 2, 3, length_x, length_y), F32),
            pltpu.VMEM((ROUNDS, 4, 8, length_y), F32),
            pltpu.VMEM((56, length_y), F32),
            pltpu.VMEM((2, 8, 128), F32),
            pltpu.VMEM((n_wall - 1, 8, 128), F32),
            pltpu.VMEM((n_span - 1, 8, 128), F32),
            dma((2,)),
            dma((2,)),
            dma((ROUNDS, 8)),
            dma((ROUNDS, 8)),
            dma((n_wall - 1,)),
            dma((n_wall - 1,)),
            dma((n_span - 1,)),
            dma((n_span - 1,)),
        ],
        compiler_params=pltpu.CompilerParams(
            collective_id=0, has_side_effects=True, vmem_limit_bytes=48 * 1024 * 1024
        ),
    )(
        velocity_old,
        heights.reshape(1, -1),
        owner_device.reshape(1, -1),
        owner_element.reshape(1, -1),
        ref_coords,
        roughness.reshape(1, -1),
        plane_hi,
        plane_lo,
        jnp.asarray(lines, F32),
        jnp.asarray(columns, F32),
    )


def solution(mesh):
    placed = (
        P(None, "wall", "span", None),
        P(),
        P(("wall", "span"), None),
        P(("wall", "span"), None),
        P(None, ("wall", "span")),
        P(("wall", "span")),
    )
    return jax.shard_map(
        functools.partial(body, mesh.shape["wall"], mesh.shape["span"]),
        mesh=mesh,
        in_specs=placed,
        out_specs=(P(None, "wall", "span", None), P(None, ("wall", "span"))),
        check_vma=False,
    )
```

time: 413 us -> 46.5 us (0.11); the launches traced: 405 us -> 46.2 us
  local copies, waits for them, and re-layouts: 126 us -> 7.51 us
  blocking collectives: 118 us -> 0 us
  other arithmetic: 73.3 us -> 0 us
  Pallas kernels: 0 us -> 38 us
  matrix products: 33.8 us -> 0 us
  starting transfers between devices: 32.8 us -> 0 us
  waiting for transfers between devices: 16.1 us -> 0 us
    psum x3 -> x0, blocking collectives: 118 us -> none  [paired_total(): return lax.psum((first, second), ('wall', 'span'))]
    pallas_call x0 -> x1, Pallas kernels: none -> 38 us  [body(): pl.pallas_call(functools.partial(kernel, n_wall, n_span, sizes), out_shap...]
    dot_general x9 -> x0, matrix products: 33.8 us -> none  [the longest x3 21 us: operate(): along_y = jnp.einsum('cxzb,ab->cxza', field, stiff_y, precision=precise)]
    ppermute x20 -> x0, starting transfers between devices: 32.8 us -> none  [the longest x8 19.2 us: with_halo(): lax.ppermute(head, axis, [((i + 1) % count, i) for i in range(count)])]
    reshape x13 -> x0, local copies, waits for them, and re-layouts: 26.9 us -> none  [the longest x4 15 us: join_faces(): return joined.reshape(core.shape)]
    gather x28 -> x0, local copies, waits for them, and re-layouts: 17.6 us -> none  [the longest x24 15.4 us: evaluate(): values = element_rows[row_ids].reshape(row_ids.shape[0], 3, 8, 8, 8)]
    add x21 -> x0, other arithmetic: 17.4 us -> none  [the longest x12 14.2 us: join_faces(): first + prev_last]
    sub x30 -> x0, other arithmetic: 17 us -> none  [the longest x4 15.1 us: body(): residual = residual - spread(step_size) * along_dir]
  transfers between devices with their start and end apart: 20 -> 0, of which waited for: 13 -> 0; matrix products, arithmetic and copies ran while one was open for 11% -> 0% of each run, Pallas kernels for 0% -> 0%
where the time goes in v1:
time: 46.5 us; the launch traced here: 46.2 us
  Pallas kernels  38 us (82%)
  local copies, waits for them, and re-layouts  7.51 us (16%)
  between operations  0.68 us (1%)
    pallas_call x1, Pallas kernels, body(): pl.pallas_call(functools.partial(kernel, n_wall, n_span, sizes), out_shap...  38 us
    unnamed x22, local copies, waits for them, and re-layouts  7.51 us

profile of v1, /device:TPU:0, one launch (start us, length us, event | category | flops | bytes accessed | tf_op | source)
XLA Modules:
  0.0 46.2 jit_solution(13267115738876859263)
XLA Ops:
  0.6 0.0 copy-start.8
  0.6 0.0 copy-start.7
  0.7 0.0 copy-start.6
  0.7 0.0 copy-start.9
  0.7 0.6 %copy-done.8 = f32[512]{0:T(512)S(1)} copy-done((f32[512]{0:T(512)S(1)}, f32[512]{0:T(512)}, u32[]{:S(2)}) %copy-start.8) | copy-done | bytes 2072
  1.3 0.0 copy-done.7
  1.3 0.0 copy-done.6
  1.3 0.0 copy-done.9
  1.3 0.0 copy-start
  1.4 1.0 %copy-done = f32[3,16,16,128]{3,2,1,0:T(8,128)S(1)} copy-done((f32[3,16,16,128]{3,2,1,0:T(8,128)S(1)}, f32[3,16,16,128]{3,2,1,0:T(8,128)}, u32[]{:S(2)}) %copy-start) | copy-done | bytes 393240
  2.3 0.0 copy-start.1
  2.3 1.0 %copy-done.1 = f32[3,256,128]{2,1,0:T(8,128)S(1)} copy-done((f32[3,256,128]{2,1,0:T(8,128)S(1)}, f32[3,256,128]{2,1,0:T(8,128)}, u32[]{:S(2)}) %copy-start.1) | copy-done | bytes 393240
  3.3 0.0 copy-start.2
  3.3 0.9 %copy-done.2 = bf16[256,512]{1,0:T(8,128)(2,1)S(1)} copy-done((bf16[256,512]{1,0:T(8,128)(2,1)S(1)}, bf16[256,512]{1,0:T(8,128)(2,1)}, u32[]{:S(2)}) %copy-start.2) | copy-done | bytes 262168
  4.3 0.0 copy-start.3
  4.3 0.9 %copy-done.3 = bf16[256,512]{1,0:T(8,128)(2,1)S(1)} copy-done((bf16[256,512]{1,0:T(8,128)(2,1)S(1)}, bf16[256,512]{1,0:T(8,128)(2,1)}, u32[]{:S(2)}) %copy-start.3) | copy-done | bytes 262168
  5.2 0.0 copy-start.4
  5.2 0.9 %copy-done.4 = f32[2,128,128]{2,1,0:T(8,128)S(1)} copy-done((f32[2,128,128]{2,1,0:T(8,128)S(1)}, f32[2,128,128]{2,1,0:T(8,128)}, u32[]{:S(2)}) %copy-start.4) | copy-done | bytes 131096
  6.1 0.0 copy-start.5
  6.1 0.7 %copy-done.5 = f32[3,512]{1,0:T(4,128)S(1)} copy-done((f32[3,512]{1,0:T(4,128)S(1)}, f32[3,512]{1,0:T(4,128)}, u32[]{:S(2)}) %copy-start.5) | copy-done | bytes 6168
  6.8 38.0 %shard_map.113 = (f32[3,16,16,128]{3,2,1,0:T(8,128)S(1)}, f32[2,512]{1,0:T(2,128)S(1)}) custom-call(f32[3,16,16,128]{3,2,1,0:T(8,128)S(1)} %copy-done, f32[1,16]{1,0:T(1,128)S(1)} %bitcast.7, s32[1,512]{1,0:T(1,128)S(1)} %bitcast.4, s32[1,512]{1,0:T(1,128)S(1)} %bitcast.5, f32[3,512]{1,0:T(4,128)S(1)} %copy-done.5, f32[1,512]{1,0:T(1,128)S(1)} %bitcast.6, ...), custom_call_target="tpu_custom_call" | custom-call | tf_op jit(solution)/shard_map/pallas_call | solution.py:474
  44.8 0.7 %copy.14 = f32[3,16,16,128]{3,2,1,0:T(8,128)} copy(f32[3,16,16,128]{3,2,1,0:T(8,128)S(1)} %get-tuple-element.4) | data formatting | bytes 786432
  45.6 0.6 %copy.15 = f32[2,512]{1,0:T(2,128)} copy(f32[2,512]{1,0:T(2,128)S(1)} %get-tuple-element.5) | data formatting | bytes 8192
Async XLA Ops:
  0.6 0.7 %copy-start.8 = (f32[512]{0:T(512)S(1)}, f32[512]{0:T(512)}, u32[]{:S(2)}) copy-start(f32[512]{0:T(512)} %param.15) | copy-start | bytes 6148
  0.6 0.7 %copy-start.7 = (s32[512,1]{0,1:T(1,128)S(1)}, s32[512,1]{0,1:T(1,128)}, u32[]{:S(2)}) copy-start(s32[512,1]{0,1:T(1,128)} %param.13) | copy-start | bytes 6148
  0.7 0.7 %copy-start.6 = (s32[512,1]{0,1:T(1,128)S(1)}, s32[512,1]{0,1:T(1,128)}, u32[]{:S(2)}) copy-start(s32[512,1]{0,1:T(1,128)} %param.12) | copy-start | bytes 6148
  0.7 0.7 %copy-start.9 = (f32[16]{0:T(128)S(1)}, f32[16]{0:T(128)}, u32[]{:S(2)}) copy-start(f32[16]{0:T(128)} %param.11) | copy-start | bytes 196
  1.3 1.0 %copy-start = (f32[3,16,16,128]{3,2,1,0:T(8,128)S(1)}, f32[3,16,16,128]{3,2,1,0:T(8,128)}, u32[]{:S(2)}) copy-start(f32[3,16,16,128]{3,2,1,0:T(8,128)} %vel.1) | copy-start | bytes 1179652
  2.3 1.0 %copy-start.1 = (f32[3,256,128]{2,1,0:T(8,128)S(1)}, f32[3,256,128]{2,1,0:T(8,128)}, u32[]{:S(2)}) copy-start(f32[3,256,128]{2,1,0:T(8,128)} %constant.8.clone.columns) | copy-start | bytes 1179652
  3.3 0.9 %copy-start.2 = (bf16[256,512]{1,0:T(8,128)(2,1)S(1)}, bf16[256,512]{1,0:T(8,128)(2,1)}, u32[]{:S(2)}) copy-start(bf16[256,512]{1,0:T(8,128)(2,1)} %constant.12.plane_lo) | copy-start | bytes 786436
  4.3 0.9 %copy-start.3 = (bf16[256,512]{1,0:T(8,128)(2,1)S(1)}, bf16[256,512]{1,0:T(8,128)(2,1)}, u32[]{:S(2)}) copy-start(bf16[256,512]{1,0:T(8,128)(2,1)} %constant.9.plane_hi) | copy-start | bytes 786436
  5.2 0.9 %copy-start.4 = (f32[2,128,128]{2,1,0:T(8,128)S(1)}, f32[2,128,128]{2,1,0:T(8,128)}, u32[]{:S(2)}) copy-start(f32[2,128,128]{2,1,0:T(8,128)} %constant.7.clone.lines) | copy-start | bytes 393220
  6.1 0.7 %copy-start.5 = (f32[3,512]{1,0:T(4,128)S(1)}, f32[3,512]{1,0:T(4,128)}, u32[]{:S(2)}) copy-start(f32[3,512]{1,0:T(4,128)} %coords.1) | copy-start | bytes 18436

commit v2 on v1

--- a/solution.py
+++ b/solution.py
@@ -37,6 +37,7 @@
 element_dz = 0.13
 NEAR = 2
 ROUNDS = 3
+SINGLE_STAGE = 64
 MESH = pl.DeviceIdType.MESH
 F32 = jnp.float32
 BF16 = jnp.bfloat16
@@ -169,6 +170,18 @@
     n_wall,
     n_span,
     sizes,
+    vel_in,
+    heights_in,
+    owner_in,
+    element_in,
+    coords_in,
+    roughness_in,
+    plane_hi_in,
+    plane_lo_in,
+    lines_in,
+    columns_in,
+    out,
+    neumann,
     vel,
     heights,
     owner,
@@ -179,8 +192,7 @@
     plane_lo,
     lines,
     columns,
-    out,
-    neumann,
+    load_sem,
     near,
     near_got,
     field,
@@ -212,12 +224,37 @@
     def at(dx, dz):
         return (lax.rem(w + (dx + n_wall), n_wall), lax.rem(s + (dz + n_span), n_span))
 
-    greeted = [(k, 0) for k in range(1, n_wall)] + [(0, k) for k in range(1, n_span)]
-    greeted += list(DIRS)
+    loads = [
+        pltpu.make_async_copy(source, target, load_sem.at[index])
+        for index, (source, target) in enumerate(
+            (
+                (vel_in, vel),
+                (heights_in, heights),
+                (lines_in, lines),
+                (coords_in, coords),
+                (owner_in, owner),
+                (element_in, element),
+                (columns_in, columns),
+                (roughness_in, roughness),
+                (plane_hi_in, plane_hi),
+                (plane_lo_in, plane_lo),
+            )
+        )
+    ]
+    for load in loads:
+        load.start()
+
+    single = n_wall * n_span <= SINGLE_STAGE
+    if single:
+        greeted = [divmod(k, n_span) for k in range(1, n_wall * n_span)]
+    else:
+        greeted = [(k, 0) for k in range(1, n_wall)] + [(0, k) for k in range(1, n_span)]
+        greeted += list(DIRS)
     barrier = pltpu.get_barrier_semaphore()
     for dx, dz in greeted:
         pl.semaphore_signal(barrier, inc=1, device_id=at(dx, dz), device_id_type=MESH)
 
+    loads[0].wait()
     lane = lax.broadcasted_iota(jnp.int32, (64, length_y), 1)
     groups = (length_x // 8) * count_z
     for index, comp in enumerate((0, 2)):
@@ -246,6 +283,8 @@
         copy.start()
         near_copies.append(copy)
 
+    for load in loads[1:]:
+        load.wait()
     layer_of = lax.broadcasted_iota(jnp.int32, (length_y, count_y), 0) // 8
     layer = lax.broadcasted_iota(jnp.int32, (length_y, count_y), 1)
     height_row = heights[...]
@@ -429,13 +468,16 @@
             copies.append(copy)
         for copy in copies:
             copy.wait()
-        total = row
-        for k in range(1, count):
-            total = total + got[k - 1, 0:1, :]
-        return total
-
-    row = gather_sum(0, row, n_wall, wall_got, wall_ss, wall_rs, lambda k: at(k, 0))
-    row = gather_sum(1, row, n_span, span_got, span_ss, span_rs, lambda k: at(0, k))
+        return row + jnp.sum(got[...], axis=0)[0:1]
+
+    if single:
+        every = n_wall * n_span
+        row = gather_sum(
+            0, row, every, wall_got, wall_ss, wall_rs, lambda k: at(k // n_span, k % n_span)
+        )
+    else:
+        row = gather_sum(0, row, n_wall, wall_got, wall_ss, wall_rs, lambda k: at(k, 0))
+        row = gather_sum(1, row, n_span, span_got, span_ss, span_rs, lambda k: at(0, k))
     totals = jnp.sum(jnp.where(diagonal, row, 0.0), axis=1, keepdims=True)
     m00, m01, m11, m02, m12, m22, e22 = [totals[q * 8 : q * 8 + 8, :] for q in range(7)]
     t1, t2 = shifts
@@ -469,7 +511,22 @@
     points = owner_device.shape[0]
     both, lines, columns = tables(*sizes)
     plane_hi, plane_lo = split_np(both)
+    every = n_wall * n_span
+    first = every if every <= SINGLE_STAGE else n_wall
     vmem = pl.BlockSpec(memory_space=pltpu.VMEM)
+    hbm = pl.BlockSpec(memory_space=pltpu.HBM)
+    operands = (
+        velocity_old,
+        heights.reshape(1, -1),
+        owner_device.reshape(1, -1),
+        owner_element.reshape(1, -1),
+        ref_coords,
+        roughness.reshape(1, -1),
+        plane_hi,
+        plane_lo,
+        jnp.asarray(lines, F32),
+        jnp.asarray(columns, F32),
+    )
     dma = pltpu.SemaphoreType.DMA
     return pl.pallas_call(
         functools.partial(kernel, n_wall, n_span, sizes),
@@ -477,9 +534,11 @@
             jax.ShapeDtypeStruct(velocity_old.shape, F32),
             jax.ShapeDtypeStruct((2, points), F32),
         ),
-        in_specs=[vmem] * 10,
+        in_specs=[hbm] * 10,
         out_specs=(vmem, vmem),
-        scratch_shapes=[
+        scratch_shapes=[pltpu.VMEM(value.shape, value.dtype) for value in operands]
+        + [
+            dma((10,)),
             pltpu.VMEM((2, 64, length_y), F32),
             pltpu.VMEM((2, 2, 64, length_y), F32),
             pltpu.VMEM((3, 3, rows, length_y), F32),
@@ -491,32 +550,21 @@
             pltpu.VMEM((ROUNDS, 4, 8, length_y), F32),
             pltpu.VMEM((56, length_y), F32),
             pltpu.VMEM((2, 8, 128), F32),
-            pltpu.VMEM((n_wall - 1, 8, 128), F32),
+            pltpu.VMEM((first - 1, 8, 128), F32),
             pltpu.VMEM((n_span - 1, 8, 128), F32),
             dma((2,)),
             dma((2,)),
             dma((ROUNDS, 8)),
             dma((ROUNDS, 8)),
-            dma((n_wall - 1,)),
-            dma((n_wall - 1,)),
+            dma((first - 1,)),
+            dma((first - 1,)),
             dma((n_span - 1,)),
             dma((n_span - 1,)),
         ],
         compiler_params=pltpu.CompilerParams(
-            collective_id=0, has_side_effects=True, vmem_limit_bytes=48 * 1024 * 1024
+            collective_id=0, has_side_effects=True, vmem_limit_bytes=67043328
         ),
-    )(
-        velocity_old,
-        heights.reshape(1, -1),
-        owner_device.reshape(1, -1),
-        owner_element.reshape(1, -1),
-        ref_coords,
-        roughness.reshape(1, -1),
-        plane_hi,
-        plane_lo,
-        jnp.asarray(lines, F32),
-        jnp.asarray(columns, F32),
-    )
+    )(*operands)
 
 
 def solution(mesh):

time: 46.5 us -> 41.6 us (0.89)
  local copies, waits for them, and re-layouts: 7.51 us -> 2.36 us
  Pallas kernels: 38 us -> 38.5 us
    unnamed x22 -> x4, local copies, waits for them, and re-layouts: 7.51 us -> 2.36 us
    pallas_call x1, Pallas kernels: 38 us -> 38.5 us  [body(): pl.pallas_call(functools.partial(kernel, n_wall, n_span, sizes), out_shap...]
where the time goes in v2:
time: 41.6 us; the launch traced here: 41.5 us
  Pallas kernels  38.5 us (93%)
  local copies, waits for them, and re-layouts  2.36 us (6%)
  between operations  0.65 us (2%)
    pallas_call x1, Pallas kernels, body(): pl.pallas_call(functools.partial(kernel, n_wall, n_span, sizes), out_shap...  38.5 us
    unnamed x4, local copies, waits for them, and re-layouts  2.36 us

profile of v2, /device:TPU:0, one launch (start us, length us, event | category | flops | bytes accessed | tf_op | source)
XLA Modules:
  0.0 41.5 jit_solution(17723910315200460287)
XLA Ops:
  0.6 38.5 %shard_map.113 = (f32[3,16,16,128]{3,2,1,0:T(8,128)}, f32[2,512]{1,0:T(2,128)}) custom-call(f32[3,16,16,128]{3,2,1,0:T(8,128)} %vel_in.1, f32[1,16]{1,0:T(1,128)} %bitcast.7, s32[1,512]{1,0:T(1,128)} %bitcast.4, s32[1,512]{1,0:T(1,128)} %bitcast.5, f32[3,512]{1,0:T(4,128)} %coords_in.1, f32[1,512]{1,0:T(1,128)} %bitcast.6, ...), custom_call_target="tpu_custom_call" | custom-call | tf_op jit(solution)/shard_map/pallas_call | solution.py:531
  39.1 0.0 copy-start
  39.1 1.8 %copy.14 = f32[3,16,16,128]{3,2,1,0:T(8,128)} copy(f32[3,16,16,128]{3,2,1,0:T(8,128)} %get-tuple-element.4) | data formatting | bytes 786432
  40.9 0.0 copy-done
  40.9 0.6 %copy.15 = f32[2,512]{1,0:T(2,128)} copy(f32[2,512]{1,0:T(2,128)S(1)} %copy-done) | data formatting | bytes 8192
Async XLA Ops:
  39.1 1.8 %copy-start = (f32[2,512]{1,0:T(2,128)S(1)}, f32[2,512]{1,0:T(2,128)}, u32[]{:S(2)}) copy-start(f32[2,512]{1,0:T(2,128)} %get-tuple-element.5) | copy-start | bytes 12292

commit v3 on v2

--- a/solution.py
+++ b/solution.py
@@ -36,7 +36,23 @@
 element_dx = 0.05
 element_dz = 0.13
 NEAR = 2
-ROUNDS = 3
+ROUNDS = 2
+REACH = 2
+TERMS = (
+    (0, 0, 0),
+    (1, 1, 2),
+    (1, 2, 1),
+    (2, 2, 2),
+    (3, 3, 6),
+    (3, 4, 5),
+    (3, 5, 4),
+    (3, 6, 3),
+    (4, 4, 6),
+    (4, 6, 4),
+    (5, 5, 6),
+    (5, 6, 5),
+    (6, 6, 6),
+)
 SINGLE_STAGE = 64
 MESH = pl.DeviceIdType.MESH
 F32 = jnp.float32
@@ -110,14 +126,12 @@
     lines_mass = np.tile(0.5 * weights, count_y)[:, None] * join_y
     lines_stiff = viscosity * 2.0 * (np.kron(np.eye(count_y), stiffness) @ join_y)
     lines = np.stack([lines_mass, lines_stiff])
-    full = np.tile(mass_x, 3)
     ring_x = join_matrix(length_x) @ mass_x
     ring_z = join_matrix(length_z) @ mass_z
     ring_x[0] *= 2.0
     ring_x[-1] *= 2.0
     ring_z[0] *= 2.0
     ring_z[-1] *= 2.0
-    del full
     assembled = inverse_step * np.kron(ring_x, ring_z)
     inner_x = face_weights(length_x, True)
     inner_z = face_weights(length_z, True)
@@ -131,7 +145,31 @@
             np.kron(inner_x, inner_z)[:, None] * weight_y[None],
         ]
     )
-    return both, lines, columns
+    reach = 2 * REACH + 1
+
+    def words(length, mass, stiff, extra):
+        size = reach * length
+        join = join_matrix(size)
+        light = join @ np.diag(np.tile(mass, reach))
+        heavy = viscosity * join @ np.kron(np.eye(size // 8), stiff) + extra * light
+        chains = [
+            light,
+            heavy @ light,
+            light @ light,
+            heavy @ heavy @ light,
+            heavy @ light @ light,
+            light @ heavy @ light,
+            light @ light @ light,
+        ]
+        middle = REACH * length
+        chains = [chain[middle : middle + length] for chain in chains]
+        return np.concatenate(chains + [np.zeros((128 - 7 * length, size))], axis=0)
+
+    words_x = words(length_x, mass_x, stiffness * (2.0 / element_dx), 0.0)
+    words_z = words(length_z, mass_z, stiffness * (2.0 / element_dz), inverse_step)
+    pad = np.zeros((128, 128 - reach * length_z))
+    words_z = np.concatenate([words_z, pad], axis=1)
+    return both, lines, columns, words_x, words_z
 
 
 def split(value):
@@ -180,6 +218,8 @@
     plane_lo_in,
     lines_in,
     columns_in,
+    words_x_in,
+    words_z_in,
     out,
     neumann,
     vel,
@@ -192,6 +232,8 @@
     plane_lo,
     lines,
     columns,
+    words_x,
+    words_z,
     load_sem,
     near,
     near_got,
@@ -206,6 +248,10 @@
     sum_send,
     wall_got,
     span_got,
+    pull_send,
+    pull_got,
+    pull_ss,
+    pull_rs,
     near_ss,
     near_rs,
     face_ss,
@@ -238,6 +284,8 @@
                 (roughness_in, roughness),
                 (plane_hi_in, plane_hi),
                 (plane_lo_in, plane_lo),
+                (words_x_in, words_x),
+                (words_z_in, words_z),
             )
         )
     ]
@@ -249,7 +297,15 @@
         greeted = [divmod(k, n_span) for k in range(1, n_wall * n_span)]
     else:
         greeted = [(k, 0) for k in range(1, n_wall)] + [(0, k) for k in range(1, n_span)]
-        greeted += list(DIRS)
+        greeted += sorted(
+            {
+                ((dx + n_wall) % n_wall, (dz + n_span) % n_span)
+                for dx in range(-REACH, REACH + 1)
+                for dz in range(-REACH, REACH + 1)
+            }
+            - {(0, 0)}
+            - set(greeted)
+        )
     barrier = pltpu.get_barrier_semaphore()
     for dx, dz in greeted:
         pl.semaphore_signal(barrier, inc=1, device_id=at(dx, dz), device_id_type=MESH)
@@ -298,43 +354,6 @@
     scale = columns[0] * mass_row
     for c in range(3):
         field[0, c] = vel[c].reshape(rows, length_y) * scale
-
-    points = owner.shape[1]
-    row_x = lagrange_rows(coords[0:1, :])
-    row_z = lagrange_rows(coords[1:2, :])
-    row_y = lagrange_rows(coords[2:3, :])
-    cross = jnp.concatenate([row_x[a : a + 1] * row_z for a in range(8)], axis=0)
-    distance = lax.rem(owner[...] - w + n_wall, n_wall)
-    from_next = distance == 1
-    from_prev = distance == n_wall - 1
-    own = jnp.logical_not(jnp.logical_or(from_next, from_prev))
-    spread = jnp.concatenate(
-        [jnp.where(mask, cross, 0.0) for mask in (own, from_prev, from_next)], axis=0
-    )
-    n_row = lax.broadcasted_iota(jnp.int32, (length_y, points), 0)
-    within = (n_row % 32) // 8
-    layer_y = jnp.where(within < NEAR, within + (count_y - NEAR), within - NEAR)
-    wanted = (n_row // 32) * count_y + layer_y == element[...]
-    along = jnp.where(wanted, jnp.concatenate([row_y] * (length_y // 8), axis=0), 0.0)
-    spread = split(spread)
-
-    for copy in near_copies:
-        copy.wait()
-
-    sampled = []
-    for index in range(2):
-        sources = jnp.concatenate(
-            [near[index], near_got[0, index], near_got[1, index]], axis=0
-        )
-        values = dot3(split(sources), spread, TN)
-        sampled.append(jnp.sum(values * along, axis=0, keepdims=True))
-    stream, spanwise = sampled
-    speed = jnp.sqrt(stream * stream + spanwise * spanwise + speed_floor)
-    drag = karman / jnp.log(sample_height / roughness[...])
-    factor = -(drag * drag * speed / viscosity)
-    gradient = (factor * stream, factor * spanwise)
-    neumann[0:1, :] = gradient[0]
-    neumann[1:2, :] = gradient[1]
 
     def face_copies(turn):
         copies = []
@@ -395,34 +414,18 @@
         for c in range(3):
             for slot, dx in enumerate((1, -1)):
                 start = 0 if dx == 1 else rows - length_z
-                field[turn, c, pl.ds(start, length_z), :] += x_got[turn, slot, c]
+                field[turn + 1, c, pl.ds(start, length_z), :] += x_got[turn, slot, c]
             for slot, dz in enumerate((1, -1)):
                 edge = pl.ds(0 if dz == 1 else length_z - 1, length_x, stride=length_z)
-                field[turn, c, edge, :] = field[turn, c, edge, :] + z_got[turn, slot, c]
+                field[turn + 1, c, edge, :] = field[turn + 1, c, edge, :] + z_got[turn, slot, c]
             for slot, (dx, dz) in enumerate(DIRS):
                 at_row = corner(-dx, -dz)
-                field[turn, c, at_row : at_row + 1, :] += c_got[turn, slot, c : c + 1, :]
+                field[turn + 1, c, at_row : at_row + 1, :] += c_got[turn, slot, c : c + 1, :]
 
     def inner(quantity, c, product):
         parts[quantity * 8 + c : quantity * 8 + c + 1, :] = jnp.sum(
             product, axis=0, keepdims=True
         )
-
-    n_line = lax.broadcasted_iota(jnp.int32, (length_y, rows), 0)
-    mass_hi = plane_hi[:, rows:]
-    mass_lo = plane_lo[:, rows:]
-    for index, c in enumerate((0, 2)):
-        pull = viscosity * gradient[index]
-        lifted = jnp.where(
-            n_line == 0, pull[:, :rows], jnp.where(n_line == length_y - 1, pull[:, rows:], 0.0)
-        )
-        local[0, c] = dot3((mass_hi, mass_lo), split(lifted), NT)
-    local[0, 1] = jnp.zeros((rows, length_y), F32)
-    copies = send_faces(0)
-    parts[...] = jnp.zeros_like(parts)
-    for c in (0, 2):
-        field[0, c] += local[0, c]
-    add_faces(0, copies)
 
     def operate(source, target):
         for c in range(3):
@@ -438,17 +441,188 @@
             for other in range(newest + 1):
                 inner(slots[(other, newest)], c, weighted * field[other, c])
 
-    for turn in (1, 2):
-        operate(turn - 1, turn)
-        copies = send_faces(turn)
-        for c in range(3):
-            field[turn, c] = local[turn, c] - shifts[turn - 1] * field[turn - 1, c]
-        inner_products(turn - 1)
-        add_faces(turn, copies)
-    operate(2, 3)
-    inner_products(2)
+    operate(0, 0)
+    copies_one = send_faces(0)
     for c in range(3):
-        inner(6, c, field[2, c] * columns[2] * local[3, c])
+        field[1, c] = local[0, c]
+    parts[...] = jnp.zeros_like(parts)
+
+    points = owner.shape[1]
+    row_x = lagrange_rows(coords[0:1, :])
+    row_z = lagrange_rows(coords[1:2, :])
+    row_y = lagrange_rows(coords[2:3, :])
+    cross = jnp.concatenate([row_x[a : a + 1] * row_z for a in range(8)], axis=0)
+    distance = lax.rem(owner[...] - w + n_wall, n_wall)
+    from_next = distance == 1
+    from_prev = distance == n_wall - 1
+    own = jnp.logical_not(jnp.logical_or(from_next, from_prev))
+    spread = jnp.concatenate(
+        [jnp.where(mask, cross, 0.0) for mask in (own, from_prev, from_next)], axis=0
+    )
+    n_row = lax.broadcasted_iota(jnp.int32, (length_y, points), 0)
+    within = (n_row % 32) // 8
+    layer_y = jnp.where(within < NEAR, within + (count_y - NEAR), within - NEAR)
+    wanted = (n_row // 32) * count_y + layer_y == element[...]
+    along = jnp.where(wanted, jnp.concatenate([row_y] * (length_y // 8), axis=0), 0.0)
+    spread = split(spread)
+
+    for copy in near_copies:
+        copy.wait()
+
+    sampled = []
+    for index in range(2):
+        sources = jnp.concatenate(
+            [near[index], near_got[0, index], near_got[1, index]], axis=0
+        )
+        values = dot3(split(sources), spread, TN)
+        sampled.append(jnp.sum(values * along, axis=0, keepdims=True))
+    stream, spanwise = sampled
+    speed = jnp.sqrt(stream * stream + spanwise * spanwise + speed_floor)
+    drag = karman / jnp.log(sample_height / roughness[...])
+    factor = -(drag * drag * speed / viscosity)
+    gradient = (factor * stream, factor * spanwise)
+    neumann[0:1, :] = gradient[0]
+    neumann[1:2, :] = gradient[1]
+
+    planes = []
+    for index in range(2):
+        pull = viscosity * gradient[index]
+        planes += [pull[:, :rows], pull[:, rows:]]
+    node = lax.broadcasted_iota(jnp.int32, (length_x, rows), 1) // length_z
+    node_row = lax.broadcasted_iota(jnp.int32, (length_x, rows), 0)
+    masked = jnp.concatenate([jnp.where(node == node_row, plane, 0.0) for plane in planes], axis=0)
+    pick_row = lax.broadcasted_iota(jnp.int32, (rows, 128), 0)
+    pick_lane = lax.broadcasted_iota(jnp.int32, (rows, 128), 1)
+    pick = jnp.where(lax.rem(pick_row, length_z) == pick_lane, 1.0, 0.0).astype(BF16)
+    masked_hi, masked_lo = split(masked)
+    flat = jnp.dot(masked_hi, pick, preferred_element_type=F32) + jnp.dot(
+        masked_lo, pick, preferred_element_type=F32
+    )
+    bundle = flat[0:8]
+    tiles = 4 * length_x // 8
+    for tile in range(1, tiles):
+        bundle = bundle + pltpu.roll(flat[tile * 8 : tile * 8 + 8], tile * length_z, 1)
+    pull_send[...] = bundle
+    reach = 2 * REACH + 1
+    pull_copies = []
+    for dx in range(-REACH, REACH + 1):
+        for dz in range(-REACH, REACH + 1):
+            if (dx, dz) == (0, 0):
+                continue
+            slot = (REACH - dx) * reach + (REACH - dz)
+            copy = remote(
+                pull_send, pull_got.at[slot], pull_ss.at[slot], pull_rs.at[slot], at(dx, dz)
+            )
+            copy.start()
+            pull_copies.append(copy)
+
+    add_faces(0, copies_one)
+    operate(1, 1)
+    copies_two = send_faces(1)
+    for c in range(3):
+        field[2, c] = local[1, c]
+    lines_rows = jnp.concatenate([lines_mass, lines[1] / height], axis=1)
+    ends = [lines_rows[0:1], lines_rows[length_y - 1 : length_y]]
+    once = [(end[:, :length_y], end[:, length_y:]) for end in ends]
+    twice = dot3(
+        split(jnp.concatenate([once[0][0], once[0][1], once[1][0], once[1][1]] * 2, axis=0)),
+        (lines_hi, lines_lo),
+        NN,
+    )
+    one_lane = lax.broadcasted_iota(jnp.int32, (1, length_y), 1)
+    zero = jnp.zeros((1, length_y), F32)
+    images = []
+    for side in range(2):
+        tip = jnp.where(one_lane == side * (length_y - 1), 1.0, 0.0)
+        by_mass, by_stiff = twice[2 * side : 2 * side + 1], twice[2 * side + 1 : 2 * side + 2]
+        rows_of = [
+            (tip, zero, zero),
+            (zero, once[side][0], zero),
+            (zero, once[side][1], zero),
+            (zero, zero, by_mass[:, :length_y]),
+            (zero, zero, by_stiff[:, :length_y]),
+            (zero, zero, by_mass[:, length_y:]),
+            (zero, zero, by_stiff[:, length_y:]),
+        ]
+        for entry in rows_of:
+            image = jnp.concatenate(entry, axis=1)
+            images.append(jnp.broadcast_to(image, (length_z, 3 * length_y)))
+        images.append(jnp.zeros((128 - 7 * length_z, 3 * length_y), F32))
+    images = split(jnp.concatenate(images, axis=0))
+    words_x_parts = split(words_x[...])
+    words_z_parts = split(words_z[...])
+
+    for copy in pull_copies:
+        copy.wait()
+    small_lane = lax.broadcasted_iota(jnp.int32, (8, 128), 1) // length_z
+    spans = []
+    for ix in range(reach):
+        pieces = [
+            bundle if (ix, iz) == (REACH, REACH) else pull_got[ix * reach + iz]
+            for iz in range(reach)
+        ]
+        for tile in range(tiles):
+            line = jnp.zeros((8, 128), F32)
+            for iz in range(reach):
+                shift = ((iz - tile) * length_z) % 128
+                moved = pltpu.roll(pieces[iz], shift, 1) if shift else pieces[iz]
+                line = jnp.where(small_lane == iz, moved, line)
+            spans.append(line)
+    along_z = dot3(split(jnp.concatenate(spans, axis=0)), words_z_parts, NT)
+    by_plane = []
+    for plane in range(4):
+        by_plane.append(
+            jnp.concatenate(
+                [
+                    along_z[(ix * 4 + plane) * length_x : (ix * 4 + plane + 1) * length_x]
+                    for ix in range(reach)
+                ],
+                axis=0,
+            )
+        )
+    both_ways = dot3(words_x_parts, split(jnp.concatenate(by_plane, axis=1)), NN)
+    block_lane = lax.broadcasted_iota(jnp.int32, (length_x, 128), 1) // length_z
+    keep_row = lax.rem(lax.broadcasted_iota(jnp.int32, (rows, 256), 0), length_z)
+    keep_lane = lax.rem(lax.broadcasted_iota(jnp.int32, (rows, 256), 1), length_z)
+    tractions = []
+    for index in range(2):
+        blocks = []
+        for side in range(2):
+            plane = index * 2 + side
+            total = jnp.zeros((length_x, 128), F32)
+            for block, word_x, word_z in TERMS:
+                piece = both_ways[
+                    word_x * length_x : (word_x + 1) * length_x, plane * 128 : plane * 128 + 128
+                ]
+                shift = ((block - word_z) * length_z) % 128
+                moved = pltpu.roll(piece, shift, 1) if shift else piece
+                total = total + jnp.where(block_lane == block, moved, 0.0)
+            blocks.append(total)
+        wide = jnp.concatenate(blocks, axis=1)
+        tall = jnp.concatenate(
+            [jnp.broadcast_to(wide[x : x + 1], (length_z, 256)) for x in range(length_x)], axis=0
+        )
+        tall = jnp.where(keep_row == keep_lane, tall, 0.0)
+        tractions.append(dot3(split(tall), images, NN))
+    add_faces(1, copies_two)
+    t1, t2 = shifts
+    for c in range(3):
+        chain = [field[level, c] for level in range(3)]
+        if c != 1:
+            taus = tractions[c // 2]
+            chain = [
+                chain[level] + taus[:, level * length_y : (level + 1) * length_y]
+                for level in range(3)
+            ]
+        v1 = chain[1] - t1 * chain[0]
+        field[0, c] = chain[0]
+        field[1, c] = v1
+        field[2, c] = chain[2] - t1 * chain[1] - t2 * v1
+    operate(2, 2)
+    for newest in range(3):
+        inner_products(newest)
+    for c in range(3):
+        inner(6, c, field[2, c] * columns[2] * local[2, c])
 
     total_rows = parts.shape[0]
     r_iota = lax.broadcasted_iota(jnp.int32, (total_rows, 128), 0)
@@ -509,7 +683,7 @@
     length_x, length_z, length_y = sizes
     rows = length_x * length_z
     points = owner_device.shape[0]
-    both, lines, columns = tables(*sizes)
+    both, lines, columns, words_x, words_z = tables(*sizes)
     plane_hi, plane_lo = split_np(both)
     every = n_wall * n_span
     first = every if every <= SINGLE_STAGE else n_wall
@@ -526,6 +700,8 @@
         plane_lo,
         jnp.asarray(lines, F32),
         jnp.asarray(columns, F32),
+        jnp.asarray(words_x, F32),
+        jnp.asarray(words_z, F32),
     )
     dma = pltpu.SemaphoreType.DMA
     return pl.pallas_call(
@@ -534,15 +710,15 @@
             jax.ShapeDtypeStruct(velocity_old.shape, F32),
             jax.ShapeDtypeStruct((2, points), F32),
         ),
-        in_specs=[hbm] * 10,
+        in_specs=[hbm] * 12,
         out_specs=(vmem, vmem),
         scratch_shapes=[pltpu.VMEM(value.shape, value.dtype) for value in operands]
         + [
-            dma((10,)),
+            dma((12,)),
             pltpu.VMEM((2, 64, length_y), F32),
             pltpu.VMEM((2, 2, 64, length_y), F32),
             pltpu.VMEM((3, 3, rows, length_y), F32),
-            pltpu.VMEM((4, 3, rows, length_y), F32),
+            pltpu.VMEM((3, 3, rows, length_y), F32),
             pltpu.VMEM((ROUNDS, 2, 3, length_x, length_y), F32),
             pltpu.VMEM((ROUNDS, 4, 8, length_y), F32),
             pltpu.VMEM((ROUNDS, 2, 3, length_z, length_y), F32),
@@ -552,6 +728,10 @@
             pltpu.VMEM((2, 8, 128), F32),
             pltpu.VMEM((first - 1, 8, 128), F32),
             pltpu.VMEM((n_span - 1, 8, 128), F32),
+            pltpu.VMEM((8, 128), F32),
+            pltpu.VMEM((25, 8, 128), F32),
+            dma((25,)),
+            dma((25,)),
             dma((2,)),
             dma((2,)),
             dma((ROUNDS, 8)),

time: 41.6 us -> 32.6 us (0.78)
  Pallas kernels: 38.5 us -> 29.4 us
    pallas_call x1, Pallas kernels: 38.5 us -> 29.4 us  [body(): pl.pallas_call(functools.partial(kernel, n_wall, n_span, sizes), out_shap...]
where the time goes in v3:
time: 32.6 us; the launch traced here: 32.5 us
  Pallas kernels  29.4 us (90%)
  local copies, waits for them, and re-layouts  2.36 us (7%)
  between operations  0.65 us (2%)
    pallas_call x1, Pallas kernels, body(): pl.pallas_call(functools.partial(kernel, n_wall, n_span, sizes), out_shap...  29.4 us
    unnamed x4, local copies, waits for them, and re-layouts  2.36 us

profile of v3, /device:TPU:0, one launch (start us, length us, event | category | flops | bytes accessed | tf_op | source)
XLA Modules:
  0.0 32.5 jit_solution(7480303899313573633)
XLA Ops:
  0.6 29.4 %shard_map.131 = (f32[3,16,16,128]{3,2,1,0:T(8,128)}, f32[2,512]{1,0:T(2,128)}) custom-call(f32[3,16,16,128]{3,2,1,0:T(8,128)} %vel_in.1, f32[1,16]{1,0:T(1,128)} %bitcast.7, s32[1,512]{1,0:T(1,128)} %bitcast.4, s32[1,512]{1,0:T(1,128)} %bitcast.5, f32[3,512]{1,0:T(4,128)} %coords_in.1, f32[1,512]{1,0:T(1,128)} %bitcast.6, ...), custom_call_target="tpu_custom_call" | custom-call | tf_op jit(solution)/shard_map/pallas_call | solution.py:707
  30.1 0.0 copy-start
  30.1 1.8 %copy.16 = f32[3,16,16,128]{3,2,1,0:T(8,128)} copy(f32[3,16,16,128]{3,2,1,0:T(8,128)} %get-tuple-element.4) | data formatting | bytes 786432
  31.9 0.0 copy-done
  31.9 0.6 %copy.17 = f32[2,512]{1,0:T(2,128)} copy(f32[2,512]{1,0:T(2,128)S(1)} %copy-done) | data formatting | bytes 8192
Async XLA Ops:
  30.1 1.8 %copy-start = (f32[2,512]{1,0:T(2,128)S(1)}, f32[2,512]{1,0:T(2,128)}, u32[]{:S(2)}) copy-start(f32[2,512]{1,0:T(2,128)} %get-tuple-element.5) | copy-start | bytes 12292

commit v4 on v3

--- a/solution.py
+++ b/solution.py
@@ -321,7 +321,22 @@
             moved = pltpu.roll(block, (group * 32 + 16) % length_y, 1)
             packed = jnp.where(lane // 32 == group, moved, packed)
         near[index] = packed
-    pl.semaphore_wait(barrier, len(greeted))
+    for load in loads[1:]:
+        load.wait()
+
+    layer_of = lax.broadcasted_iota(jnp.int32, (length_y, count_y), 0) // 8
+    layer = lax.broadcasted_iota(jnp.int32, (length_y, count_y), 1)
+    height_row = heights[...]
+    height = jnp.sum(jnp.where(layer_of == layer, height_row, 0.0), axis=1, keepdims=True)
+    lines_mass = height * lines[0]
+    lines_hi, lines_lo = split(jnp.concatenate([lines_mass, lines[1] / height], axis=1))
+    bound = jnp.max(0.1535 * height_row + 0.000182 / height_row, axis=1, keepdims=True)
+    shifts = (0.15 * bound, 0.85 * bound)
+
+    mass_row = jnp.sum(lines_mass, axis=0, keepdims=True)
+    scale = columns[0] * mass_row
+    for c in range(3):
+        field[0, c] = vel[c].reshape(rows, length_y) * scale
 
     def remote(src, dst, ss, rs, where):
         return pltpu.make_async_remote_copy(
@@ -332,28 +347,6 @@
             device_id=where,
             device_id_type=MESH,
         )
-
-    near_copies = []
-    for slot, dx in enumerate((1, -1)):
-        copy = remote(near, near_got.at[slot], near_ss.at[slot], near_rs.at[slot], at(dx, 0))
-        copy.start()
-        near_copies.append(copy)
-
-    for load in loads[1:]:
-        load.wait()
-    layer_of = lax.broadcasted_iota(jnp.int32, (length_y, count_y), 0) // 8
-    layer = lax.broadcasted_iota(jnp.int32, (length_y, count_y), 1)
-    height_row = heights[...]
-    height = jnp.sum(jnp.where(layer_of == layer, height_row, 0.0), axis=1, keepdims=True)
-    lines_mass = height * lines[0]
-    lines_hi, lines_lo = split(jnp.concatenate([lines_mass, lines[1] / height], axis=1))
-    bound = jnp.max(0.1535 * height_row + 0.000182 / height_row, axis=1, keepdims=True)
-    shifts = (0.15 * bound, 0.85 * bound)
-
-    mass_row = jnp.sum(lines_mass, axis=0, keepdims=True)
-    scale = columns[0] * mass_row
-    for c in range(3):
-        field[0, c] = vel[c].reshape(rows, length_y) * scale
 
     def face_copies(turn):
         copies = []
@@ -403,6 +396,10 @@
                 c_send[turn, slot, c : c + 1, :] = local[turn, c, at_row : at_row + 1, :]
         for slot in range(4):
             c_send[turn, slot, 3:8, :] = jnp.zeros((5, length_y), F32)
+        if turn == 0:
+            pl.semaphore_wait(barrier, len(greeted))
+            for copy in near_copies:
+                copy.start()
         copies = face_copies(turn)
         for copy in copies:
             copy.start()
@@ -440,6 +437,11 @@
             weighted = field[newest, c] * columns[1]
             for other in range(newest + 1):
                 inner(slots[(other, newest)], c, weighted * field[other, c])
+
+    near_copies = []
+    for slot, dx in enumerate((1, -1)):
+        copy = remote(near, near_got.at[slot], near_ss.at[slot], near_rs.at[slot], at(dx, 0))
+        near_copies.append(copy)
 
     operate(0, 0)
     copies_one = send_faces(0)
@@ -504,10 +506,11 @@
         bundle = bundle + pltpu.roll(flat[tile * 8 : tile * 8 + 8], tile * length_z, 1)
     pull_send[...] = bundle
     reach = 2 * REACH + 1
+    folded = n_span == 2 * REACH
     pull_copies = []
     for dx in range(-REACH, REACH + 1):
         for dz in range(-REACH, REACH + 1):
-            if (dx, dz) == (0, 0):
+            if (dx, dz) == (0, 0) or (folded and dz == REACH):
                 continue
             slot = (REACH - dx) * reach + (REACH - dz)
             copy = remote(
@@ -558,7 +561,9 @@
     spans = []
     for ix in range(reach):
         pieces = [
-            bundle if (ix, iz) == (REACH, REACH) else pull_got[ix * reach + iz]
+            bundle
+            if (ix, iz) == (REACH, REACH)
+            else pull_got[ix * reach + (reach - 1 if folded and iz == 0 else iz)]
             for iz in range(reach)
         ]
         for tile in range(tiles):
@@ -632,17 +637,21 @@
     row = jnp.sum(jnp.where(diagonal, summed, 0.0), axis=0, keepdims=True)
 
     def gather_sum(stage, row, count, got, ss, rs, place):
-        sum_send[stage] = jnp.broadcast_to(row, (8, 128))
+        sum_send[stage : stage + 1, :] = row
         copies = []
         for k in range(1, count):
             copy = remote(
-                sum_send.at[stage], got.at[k - 1], ss.at[k - 1], rs.at[k - 1], place(k)
+                sum_send.at[pl.ds(stage, 1), :],
+                got.at[pl.ds(k - 1, 1), :],
+                ss.at[k - 1],
+                rs.at[k - 1],
+                place(k),
             )
             copy.start()
             copies.append(copy)
         for copy in copies:
             copy.wait()
-        return row + jnp.sum(got[...], axis=0)[0:1]
+        return row + jnp.sum(got[...], axis=0, keepdims=True)
 
     if single:
         every = n_wall * n_span
@@ -725,9 +734,9 @@
             pltpu.VMEM((ROUNDS, 2, 3, length_x, length_y), F32),
             pltpu.VMEM((ROUNDS, 4, 8, length_y), F32),
             pltpu.VMEM((56, length_y), F32),
-            pltpu.VMEM((2, 8, 128), F32),
-            pltpu.VMEM((first - 1, 8, 128), F32),
-            pltpu.VMEM((n_span - 1, 8, 128), F32),
+            pltpu.VMEM((2, 128), F32),
+            pltpu.VMEM((first - 1, 128), F32),
+            pltpu.VMEM((n_span - 1, 128), F32),
             pltpu.VMEM((8, 128), F32),
             pltpu.VMEM((25, 8, 128), F32),
             dma((25,)),

time: 32.6 us -> 30.8 us (0.945)
  Pallas kernels: 29.4 us -> 27.6 us
    pallas_call x1, Pallas kernels: 29.4 us -> 27.6 us  [body(): pl.pallas_call(functools.partial(kernel, n_wall, n_span, sizes), out_shap...]
where the time goes in v4:
time: 30.8 us; the launch traced here: 30.6 us
  Pallas kernels  27.6 us (90%)
  local copies, waits for them, and re-layouts  2.36 us (8%)
  between operations  0.65 us (2%)
    pallas_call x1, Pallas kernels, body(): pl.pallas_call(functools.partial(kernel, n_wall, n_span, sizes), out_shap...  27.6 us
    unnamed x4, local copies, waits for them, and re-layouts  2.36 us

profile of v4, /device:TPU:0, one launch (start us, length us, event | category | flops | bytes accessed | tf_op | source)
XLA Modules:
  0.0 30.6 jit_solution(12419474597406439764)
XLA Ops:
  0.6 27.6 %shard_map.131 = (f32[3,16,16,128]{3,2,1,0:T(8,128)}, f32[2,512]{1,0:T(2,128)}) custom-call(f32[3,16,16,128]{3,2,1,0:T(8,128)} %vel_in.1, f32[1,16]{1,0:T(1,128)} %bitcast.7, s32[1,512]{1,0:T(1,128)} %bitcast.4, s32[1,512]{1,0:T(1,128)} %bitcast.5, f32[3,512]{1,0:T(4,128)} %coords_in.1, f32[1,512]{1,0:T(1,128)} %bitcast.6, ...), custom_call_target="tpu_custom_call" | custom-call | tf_op jit(solution)/shard_map/pallas_call | solution.py:716
  28.3 0.0 copy-start
  28.3 1.8 %copy.16 = f32[3,16,16,128]{3,2,1,0:T(8,128)} copy(f32[3,16,16,128]{3,2,1,0:T(8,128)} %get-tuple-element.4) | data formatting | bytes 786432
  30.0 0.0 copy-done
  30.0 0.6 %copy.17 = f32[2,512]{1,0:T(2,128)} copy(f32[2,512]{1,0:T(2,128)S(1)} %copy-done) | data formatting | bytes 8192
Async XLA Ops:
  28.3 1.8 %copy-start = (f32[2,512]{1,0:T(2,128)S(1)}, f32[2,512]{1,0:T(2,128)}, u32[]{:S(2)}) copy-start(f32[2,512]{1,0:T(2,128)} %get-tuple-element.5) | copy-start | bytes 12292

commit v5 on v4

--- a/solution.py
+++ b/solution.py
@@ -374,8 +374,8 @@
         for slot, (dx, dz) in enumerate(DIRS):
             copies.append(
                 remote(
-                    c_send.at[turn, slot],
-                    c_got.at[turn, slot],
+                    c_send.at[turn, slot, pl.ds(0, 3), :],
+                    c_got.at[turn, slot, pl.ds(0, 3), :],
                     face_ss.at[turn, 4 + slot],
                     face_rs.at[turn, 4 + slot],
                     at(dx, dz),
@@ -394,8 +394,6 @@
             for slot, (dx, dz) in enumerate(DIRS):
                 at_row = corner(dx, dz)
                 c_send[turn, slot, c : c + 1, :] = local[turn, c, at_row : at_row + 1, :]
-        for slot in range(4):
-            c_send[turn, slot, 3:8, :] = jnp.zeros((5, length_y), F32)
         if turn == 0:
             pl.semaphore_wait(barrier, len(greeted))
             for copy in near_copies:
@@ -425,10 +423,24 @@
         )
 
     def operate(source, target):
+        flat = field[source].reshape(3 * rows, length_y)
+        lined = dot3(split(flat), (lines_hi, lines_lo), NN)
+        wide = jnp.concatenate(
+            [
+                jnp.concatenate(
+                    [
+                        lined[c * rows : (c + 1) * rows, :length_y],
+                        lined[c * rows : (c + 1) * rows, length_y:],
+                    ],
+                    axis=0,
+                )
+                for c in range(3)
+            ],
+            axis=1,
+        )
+        result = dot3((plane_hi[...], plane_lo[...]), split(wide), NN)
         for c in range(3):
-            lined = dot3(split(field[source, c]), (lines_hi, lines_lo), NN)
-            stacked = jnp.concatenate([lined[:, :length_y], lined[:, length_y:]], axis=0)
-            local[target, c] = dot3((plane_hi[...], plane_lo[...]), split(stacked), NN)
+            local[target, c] = result[:, c * length_y : (c + 1) * length_y]
 
     slots = {(0, 0): 0, (0, 1): 1, (1, 1): 2, (0, 2): 3, (1, 2): 4, (2, 2): 5}
 
@@ -508,16 +520,19 @@
     reach = 2 * REACH + 1
     folded = n_span == 2 * REACH
     pull_copies = []
-    for dx in range(-REACH, REACH + 1):
-        for dz in range(-REACH, REACH + 1):
-            if (dx, dz) == (0, 0) or (folded and dz == REACH):
-                continue
-            slot = (REACH - dx) * reach + (REACH - dz)
-            copy = remote(
-                pull_send, pull_got.at[slot], pull_ss.at[slot], pull_rs.at[slot], at(dx, dz)
-            )
-            copy.start()
-            pull_copies.append(copy)
+    offsets = [
+        (dx, dz)
+        for dx in range(-REACH, REACH + 1)
+        for dz in range(-REACH, REACH + 1)
+        if (dx, dz) != (0, 0) and not (folded and dz == REACH)
+    ]
+    for dx, dz in sorted(offsets, key=lambda pair: -abs(pair[0]) - abs(pair[1])):
+        slot = (REACH - dx) * reach + (REACH - dz)
+        copy = remote(
+            pull_send, pull_got.at[slot], pull_ss.at[slot], pull_rs.at[slot], at(dx, dz)
+        )
+        copy.start()
+        pull_copies.append(copy)
 
     add_faces(0, copies_one)
     operate(1, 1)

time: 30.8 us -> 29.2 us (0.948)
  Pallas kernels: 27.6 us -> 26 us
    pallas_call x1, Pallas kernels: 27.6 us -> 26 us  [body(): pl.pallas_call(functools.partial(kernel, n_wall, n_span, sizes), out_shap...]
where the time goes in v5:
time: 29.2 us; the launch traced here: 29 us
  Pallas kernels  26 us (89%)
  local copies, waits for them, and re-layouts  2.36 us (8%)
  between operations  0.65 us (2%)
    pallas_call x1, Pallas kernels, body(): pl.pallas_call(functools.partial(kernel, n_wall, n_span, sizes), out_shap...  26 us
    unnamed x4, local copies, waits for them, and re-layouts  2.36 us

profile of v5, /device:TPU:0, one launch (start us, length us, event | category | flops | bytes accessed | tf_op | source)
XLA Modules:
  0.0 29.0 jit_solution(13631217772030951240)
XLA Ops:
  0.6 26.0 %shard_map.131 = (f32[3,16,16,128]{3,2,1,0:T(8,128)}, f32[2,512]{1,0:T(2,128)}) custom-call(f32[3,16,16,128]{3,2,1,0:T(8,128)} %vel_in.1, f32[1,16]{1,0:T(1,128)} %bitcast.7, s32[1,512]{1,0:T(1,128)} %bitcast.4, s32[1,512]{1,0:T(1,128)} %bitcast.5, f32[3,512]{1,0:T(4,128)} %coords_in.1, f32[1,512]{1,0:T(1,128)} %bitcast.6, ...), custom_call_target="tpu_custom_call" | custom-call | tf_op jit(solution)/shard_map/pallas_call | solution.py:731
  26.6 0.0 copy-start
  26.6 1.8 %copy.16 = f32[3,16,16,128]{3,2,1,0:T(8,128)} copy(f32[3,16,16,128]{3,2,1,0:T(8,128)} %get-tuple-element.4) | data formatting | bytes 786432
  28.4 0.0 copy-done
  28.4 0.6 %copy.17 = f32[2,512]{1,0:T(2,128)} copy(f32[2,512]{1,0:T(2,128)S(1)} %copy-done) | data formatting | bytes 8192
Async XLA Ops:
  26.6 1.8 %copy-start = (f32[2,512]{1,0:T(2,128)S(1)}, f32[2,512]{1,0:T(2,128)}, u32[]{:S(2)}) copy-start(f32[2,512]{1,0:T(2,128)} %get-tuple-element.5) | copy-start | bytes 12292
